TPU v7x, 256 devices: a whole 4x4x8 slice. The times are simulated.
256 devices in a mesh: dp: 32 (over z, y_hi, core), tensor: 8 (over x, y_lo).
Axes of the slice: x: 4, y: 4 (y_hi: 2, y_lo: 2; y = y_hi * 2 + y_lo), z: 8, core: 2. Of those that a mesh axis runs over, the one named last changes fastest.
Arguments:
- tokens: bfloat16 [128, 576, 1024], P('dp', 'tensor'), may hold values from -150 to 150
- cotangent: bfloat16 [128, 576, 1024], P('dp', 'tensor'), may hold values from -6 to 6
- dispatch_weight: bfloat16 [1024, 64], replicated, may hold values from -3 to 3
- w_in: bfloat16 [64, 1024, 4096], P('dp', None, 'tensor'), may hold values from -0.1875 to 0.1875
- w_out: bfloat16 [64, 4096, 1024], P('dp', 'tensor'), may hold values from -0.09375 to 0.09375
Outputs:
- grad_tokens: bfloat16 [128, 576, 1024], P('dp', 'tensor')
- grad_router: float32 [1024, 64], replicated
- grad_w_in: bfloat16 [64, 1024, 4096], P('dp', None, 'tensor')
- grad_w_out: bfloat16 [64, 4096, 1024], P('dp', 'tensor')
All inputs are finite; a program needn't handle non-finite values.
Results may differ from a plain program's by a relative error of at most 0.0079.
Values may be sent and summed in bfloat16 or wider, within the bound.
A program may use at most 64 MiB of HBM per device.

v0:
```python
import jax
import jax.numpy as jnp
from jax import lax
from jax.sharding import PartitionSpec as P


def split_up(x, dim, length):
    lengths = x.shape
    blocks = x.reshape(*lengths[:dim], length, lengths[dim] // length, *lengths[dim + 1 :])
    return jnp.moveaxis(blocks, dim, 0)


def summed_on_arrival(x, axis, dim):
    blocks = split_up(x, dim, lax.axis_size(axis))
    arrived = lax.all_to_all(blocks, axis, split_axis=0, concat_axis=0, tiled=True)
    return arrived.sum(axis=0)


def sent_to_all(x, axis):
    length = lax.axis_size(axis)
    return lax.all_to_all(jnp.broadcast_to(x[None], (length, *x.shape)), axis, 0, 0, tiled=True)


def laid_out(blocks, dim):
    lengths = list(blocks.shape[1:])
    lengths[dim] *= blocks.shape[0]
    return jnp.moveaxis(blocks, 0, dim).reshape(lengths)


def gathered_copies(x, axis, dim):
    blocks = sent_to_all(x, axis)
    return laid_out(blocks, dim)


def collected_together(x, axis):
    leaves = jax.tree.leaves(x)
    sequence = sorted(range(len(leaves)), key=lambda k: -leaves[k].size)
    width = (1, *leaves[sequence[0]].shape)[-1]
    lines = [
        jnp.pad(leaves[k].reshape(-1), (0, -leaves[k].size % width)).reshape(-1, width)
        for k in sequence
    ]
    both, at, found = (sent_to_all(jnp.concatenate(lines), axis), 0, {})
    for k, line in zip(sequence, lines):
        piece = both[:, at : at + len(line)].reshape(len(both), -1)
        found[k] = piece[:, : leaves[k].size].reshape(-1, *leaves[k].shape)
        at += len(line)
    numbers = iter(range(len(leaves)))
    return jax.tree.map(lambda _: found[next(numbers)], x)


def combined_pairwise(pieces, combine):
    while len(jax.tree.leaves(pieces)[0]) > 1:
        pieces = jax.vmap(combine)(
            *(jax.tree.map(lambda part: part[side::2], pieces) for side in (0, 1))
        )
    return jax.tree.map(lambda part: part[0], pieces)


def merged(x, axis, combine):
    pieces = collected_together(x, axis)
    return combined_pairwise(pieces, combine)


def over_copies(x, axis):
    return sent_to_all(x, axis).sum(axis=0)


def to_experts(partial_rows):
    shared_part = summed_on_arrival(partial_rows, "tensor", 2).astype(jnp.bfloat16)
    arrived = lax.all_to_all(shared_part, "dp", split_axis=1, concat_axis=0, tiled=True)
    result = gathered_copies(arrived, "tensor", 2)
    return result


def to_images(partial_rows):
    shared_part = summed_on_arrival(partial_rows, "tensor", 2).astype(jnp.bfloat16)
    arrived = lax.all_to_all(shared_part, "dp", split_axis=0, concat_axis=1, tiled=True)
    result = gathered_copies(arrived, "tensor", 2)
    return result


def join_stats(former, latter):
    biggest = jnp.maximum(former[0], latter[0])
    return (
        biggest,
        former[1] * jnp.exp(former[0] - biggest) + latter[1] * jnp.exp(latter[0] - biggest),
    )


def dispatch_softmax(logits):
    local_max = jnp.max(logits, axis=1)
    local_total = jnp.sum(jnp.exp(logits - local_max[:, None, :]), axis=1)
    global_max, totals = merged((local_max, local_total), "tensor", join_stats)
    exponent = jnp.exp(logits - global_max[:, None, :])
    return exponent / totals[:, None, :]


def on_device(tokens, cotangent, dispatch_weight, w_in, w_out):
    wide = jnp.float32
    logits = jnp.einsum("isd,de->ise", tokens, dispatch_weight, preferred_element_type=wide)
    dispatch = dispatch_softmax(logits)
    combine = jax.nn.softmax(logits, axis=2)
    dispatch_low = dispatch.astype(jnp.bfloat16)
    combine_low = combine.astype(jnp.bfloat16)
    slot_inputs = to_experts(
        jnp.einsum("ise,isd->ied", dispatch_low, tokens, preferred_element_type=wide)
    )
    pre_act = jnp.einsum("ied,edf->ief", slot_inputs, w_in, preferred_element_type=wide)
    hidden_act, gelu_back = jax.vjp(jax.nn.gelu, pre_act)
    hidden_low = hidden_act.astype(jnp.bfloat16)
    slot_outputs = to_images(
        jnp.einsum("ief,efd->ied", hidden_low, w_out, preferred_element_type=wide)
    )
    grad_combine = jnp.einsum("isd,ied->ise", cotangent, slot_outputs, preferred_element_type=wide)
    grad_slots_out = to_experts(
        jnp.einsum("ise,isd->ied", combine_low, cotangent, preferred_element_type=wide)
    )
    grad_hidden = jnp.einsum("ied,efd->ief", grad_slots_out, w_out, preferred_element_type=wide)
    grad_pre = gelu_back(grad_hidden)[0].astype(jnp.bfloat16)
    grad_w_out = jnp.einsum(
        "ief,ied->efd", hidden_low, grad_slots_out, preferred_element_type=wide
    ).astype(jnp.bfloat16)
    grad_w_in = jnp.einsum(
        "ied,ief->edf", slot_inputs, grad_pre, preferred_element_type=wide
    ).astype(jnp.bfloat16)
    grad_slots_in = to_images(
        jnp.einsum("ief,edf->ied", grad_pre, w_in, preferred_element_type=wide)
    )
    grad_dispatch = jnp.einsum("isd,ied->ise", tokens, grad_slots_in, preferred_element_type=wide)
    column_dot = over_copies(jnp.sum(grad_dispatch * dispatch, axis=1), "tensor")
    row_dot = jnp.sum(grad_combine * combine, axis=2, keepdims=True)
    grad_logits = (
        combine * (grad_combine - row_dot) + dispatch * (grad_dispatch - column_dot[:, None, :])
    ).astype(jnp.bfloat16)
    token_part = jnp.einsum(
        "ise,ied->isd", dispatch_low, grad_slots_in, preferred_element_type=wide
    )
    router_part = jnp.einsum(
        "ise,de->isd", grad_logits, dispatch_weight, preferred_element_type=wide
    )
    grad_tokens = (token_part + router_part).astype(jnp.bfloat16)
    local_router = jnp.einsum("isd,ise->de", tokens, grad_logits, preferred_element_type=wide)
    grad_router = lax.psum(local_router, ("dp", "tensor"))
    return (grad_tokens, grad_router, grad_w_in, grad_w_out)


def solution(mesh):
    return jax.shard_map(
        on_device,
        mesh=mesh,
        in_specs=(
            P("dp", "tensor", None),
            P("dp", "tensor", None),
            P(),
            P("dp", None, "tensor"),
            P("dp", "tensor", None),
        ),
        out_specs=(P("dp", "tensor", None), P(), P("dp", None, "tensor"), P("dp", "tensor", None)),
        check_vma=False,
    )
```

profile of v0, /device:TPU:1, one launch (start us, length us, event | category | flops | bytes accessed | tf_op | source)
XLA Modules:
  0.0 495.3 jit_solution(7292811887007530040)
XLA Ops:
  9.2 10.7 %all_to_all.110 = f32[8,1,512]{2,1,0:T(1,128)S(1)} all-to-all(f32[8,1,512]{2,1,0:T(1,128)S(1)} %reshape.63), channel_id=1, replica_groups=mesh['dp'=32,'tensor'=8] {'tensor'}, dimensions={0} | all-to-all | bytes 32768 | tf_op jit(solution)/shard_map/all_to_all | solution.py:21
  23.7 4.2 all-to-all-start.4
  31.1 10.9 %all-to-all-done.4 = f32[8,4,64,128]{3,2,1,0:T(8,128)} async-done(((f32[8,4,64,128]{3,2,1,0:T(8,128)}), f32[8,4,64,128]{3,2,1,0:T(8,128)}, u32[]{:S(2)}, u32[]{:S(2)}) %all-to-all-start.4) | async-done | bytes 1048608 | tf_op jit(solution)/shard_map/all_to_all | solution.py:15
  42.0 3.9 all-to-all-start.1
  47.9 12.2 %all-to-all-done.1 = f32[8,4,64,128]{3,2,1,0:T(8,128)S(1)} async-done(((f32[8,4,64,128]{3,2,1,0:T(8,128)}), f32[8,4,64,128]{3,2,1,0:T(8,128)S(1)}, u32[]{:S(2)}, u32[]{:S(2)}) %all-to-all-start.1) | async-done | bytes 1048608 | tf_op jit(solution)/shard_map/all_to_all | solution.py:15
  60.1 13.4 %all-to-all-start.5 = ((bf16[4,64,128]{2,0,1:T(4,128)(2,1)}), bf16[4,64,128]{2,0,1:T(4,128)(2,1)S(1)}, u32[]{:S(2)}, u32[]{:S(2)}) async-start(bf16[4,64,128]{2,0,1:T(4,128)(2,1)} %copy.87), calls=%async_computation.5 | async-start | bytes 131072 | tf_op jit(solution)/shard_map/all_to_all | solution.py:71
  74.2 9.0 %all-to-all-done.5 = bf16[4,64,128]{2,0,1:T(4,128)(2,1)S(1)} async-done(((bf16[4,64,128]{2,0,1:T(4,128)(2,1)}), bf16[4,64,128]{2,0,1:T(4,128)(2,1)S(1)}, u32[]{:S(2)}, u32[]{:S(2)}) %all-to-all-start.5) | async-done | bytes 65568 | tf_op jit(solution)/shard_map/all_to_all | solution.py:71
  83.2 3.9 all-to-all-start.2
  87.2 9.8 %all-to-all-done.2 = bf16[4,64,128]{2,0,1:T(4,128)(2,1)S(1)} async-done(((bf16[4,64,128]{2,0,1:T(4,128)(2,1)}), bf16[4,64,128]{2,0,1:T(4,128)(2,1)S(1)}, u32[]{:S(2)}, u32[]{:S(2)}) %all-to-all-start.2) | async-done | bytes 65568 | tf_op jit(solution)/shard_map/all_to_all | solution.py:71
  98.0 3.5 all-to-all-start.6
  101.5 9.0 %all-to-all-done.6 = bf16[8,128,2,128]{3,1,2,0:T(8,128)(2,1)S(1)} async-done(((bf16[8,128,2,128]{3,1,2,0:T(8,128)(2,1)}), bf16[8,128,2,128]{3,1,2,0:T(8,128)(2,1)S(1)}, u32[]{:S(2)}, u32[]{:S(2)}) %all-to-all-start.6) | async-done | bytes 524320 | tf_op jit(solution)/shard_map/all_to_all | solution.py:21
  111.5 4.1 all-to-all-start.3
  116.1 8.2 %all-to-all-done.3 = bf16[8,128,2,128]{3,1,2,0:T(8,128)(2,1)} async-done(((bf16[8,128,2,128]{3,1,2,0:T(8,128)(2,1)}), bf16[8,128,2,128]{3,1,2,0:T(8,128)(2,1)}, u32[]{:S(2)}, u32[]{:S(2)}) %all-to-all-start.3) | async-done | bytes 524320 | tf_op jit(solution)/shard_map/all_to_all | solution.py:21
  124.2 2.8 fusion.15
  128.9 4.2 all-to-all-start.7
  136.4 11.1 %all-to-all-done.7 = f32[8,128,2,128]{3,1,2,0:T(8,128)} async-done(((f32[8,128,2,128]{3,1,2,0:T(8,128)}), f32[8,128,2,128]{3,1,2,0:T(8,128)}, u32[]{:S(2)}, u32[]{:S(2)}) %all-to-all-start.7) | async-done | bytes 1048608 | tf_op jit(solution)/shard_map/all_to_all | solution.py:15
  147.5 4.2 all-to-all-start.10
  155.2 10.5 %all-to-all-done.10 = f32[8,128,2,128]{3,1,2,0:T(8,128)} async-done(((f32[8,128,2,128]{3,1,2,0:T(8,128)}), f32[8,128,2,128]{3,1,2,0:T(8,128)}, u32[]{:S(2)}, u32[]{:S(2)}) %all-to-all-start.10) | async-done | bytes 1048608 | tf_op jit(solution)/shard_map/all_to_all | solution.py:15
  165.8 6.7 %all-to-all-start.8 = ((bf16[128,2,128]{2,1,0:T(2,128)(2,1)}), bf16[128,2,128]{2,1,0:T(2,128)(2,1)}, u32[]{:S(2)}, u32[]{:S(2)}) async-start(bf16[128,2,128]{2,1,0:T(2,128)(2,1)} %copy.92), calls=%async_computation.8 | async-start | bytes 131072 | tf_op jit(solution)/shard_map/all_to_all | solution.py:78
  175.9 6.5 %all-to-all-done.8 = bf16[128,2,128]{2,1,0:T(2,128)(2,1)} async-done(((bf16[128,2,128]{2,1,0:T(2,128)(2,1)}), bf16[128,2,128]{2,1,0:T(2,128)(2,1)}, u32[]{:S(2)}, u32[]{:S(2)}) %all-to-all-start.8) | async-done | bytes 65568 | tf_op jit(solution)/shard_map/all_to_all | solution.py:78
  182.4 4.5 all-to-all-start.11
  188.5 8.4 %all-to-all-done.11 = bf16[128,2,128]{2,1,0:T(2,128)(2,1)} async-done(((bf16[128,2,128]{2,1,0:T(2,128)(2,1)}), bf16[128,2,128]{2,1,0:T(2,128)(2,1)}, u32[]{:S(2)}, u32[]{:S(2)}) %all-to-all-start.11) | async-done | bytes 65568 | tf_op jit(solution)/shard_map/all_to_all | solution.py:78
  198.7 4.1 all-to-all-start.9
  204.9 3.1 convolution_convert_fusion
  209.0 3.0 all-to-all-done.9
  212.9 4.1 all-to-all-start.12
  221.5 4.2 all-to-all-done.12
  225.7 3.7 all-to-all-start.13
  231.7 2.8 all-to-all-done.13
  237.0 2.5 convolution_bitcast_fusion.6
  239.6 2.5 fusion.2
  242.1 244.7 %all-reduce.2.cloned.1.call-done = f32[1024,64]{0,1:T(8,128)} async-done(((f32[1024,64]{0,1:T(8,128)}), f32[1024,64]{0,1:T(8,128)}) %all-reduce.2.cloned.1.call-update) | async-done | bytes 262160 | tf_op jit(solution)/shard_map/psum | solution.py:144
  (64 shorter events, 44.1 us)
Async XLA Ops:
  7.2 108.4 %copy-start = (bf16[2,1024,512]{2,1,0:T(8,128)(2,1)S(1)}, bf16[2,1024,512]{2,1,0:T(8,128)(2,1)}, u32[]{:S(2)}) copy-start(bf16[2,1024,512]{2,1,0:T(8,128)(2,1)} %param.8) | copy-start | bytes 6291460
  21.2 198.8 %copy-start.2 = (f32[4,64]{1,0:T(4,128)}, f32[4,64]{1,0:T(4,128)S(1)}, u32[]{:S(2)}) copy-start(f32[4,64]{1,0:T(4,128)S(1)} %get-tuple-element.10) | copy-start | bytes 3076
  21.2 198.8 %copy-start.3 = (f32[4,64]{1,0:T(4,128)}, f32[4,64]{1,0:T(4,128)S(1)}, u32[]{:S(2)}) copy-start(f32[4,64]{1,0:T(4,128)S(1)} %get-tuple-element.11) | copy-start | bytes 3076
  23.7 18.3 %all-to-all-start.4 = ((f32[8,4,64,128]{3,2,1,0:T(8,128)}), f32[8,4,64,128]{3,2,1,0:T(8,128)}, u32[]{:S(2)}, u32[]{:S(2)}) async-start(f32[8,4,64,128]{3,2,1,0:T(8,128)} %bitcast.137), calls=%async_computation.4 | async-start | bytes 2097152 | tf_op jit(solution)/shard_map/all_to_all | solution.py:15
  28.6 13.4 %copy-start.4 = (f32[4,72]{1,0:T(4,128)}, f32[4,72]{1,0:T(4,128)S(1)}, u32[]{:S(2)}) copy-start(f32[4,72]{1,0:T(4,128)S(1)} %get-tuple-element.14) | copy-start | bytes 3460
  42.0 18.1 %all-to-all-start.1 = ((f32[8,4,64,128]{3,2,1,0:T(8,128)}), f32[8,4,64,128]{3,2,1,0:T(8,128)S(1)}, u32[]{:S(2)}, u32[]{:S(2)}) async-start(f32[8,4,64,128]{3,2,1,0:T(8,128)} %bitcast.140), calls=%async_computation.1 | async-start | bytes 2097152 | tf_op jit(solution)/shard_map/all_to_all | solution.py:15
  60.1 23.1 %all-to-all-start.5 = ((bf16[4,64,128]{2,0,1:T(4,128)(2,1)}), bf16[4,64,128]{2,0,1:T(4,128)(2,1)S(1)}, u32[]{:S(2)}, u32[]{:S(2)}) async-start(bf16[4,64,128]{2,0,1:T(4,128)(2,1)} %copy.87), calls=%async_computation.5 | async-start | bytes 131072 | tf_op jit(solution)/shard_map/all_to_all | solution.py:71
  83.2 13.8 %all-to-all-start.2 = ((bf16[4,64,128]{2,0,1:T(4,128)(2,1)}), bf16[4,64,128]{2,0,1:T(4,128)(2,1)S(1)}, u32[]{:S(2)}, u32[]{:S(2)}) async-start(bf16[4,64,128]{2,0,1:T(4,128)(2,1)} %copy.82), calls=%async_computation.2 | async-start | bytes 131072 | tf_op jit(solution)/shard_map/all_to_all | solution.py:71
  98.0 12.6 %all-to-all-start.6 = ((bf16[8,128,2,128]{3,1,2,0:T(8,128)(2,1)}), bf16[8,128,2,128]{3,1,2,0:T(8,128)(2,1)S(1)}, u32[]{:S(2)}, u32[]{:S(2)}) async-start(bf16[8,128,2,128]{3,1,2,0:T(8,128)(2,1)} %broadcast_in_dim.24), calls=%async_computation.6 | async-start | bytes 1048576 | tf_op jit(solution)/shard_map/all_to_all | solution.py:21
  111.5 12.8 %all-to-all-start.3 = ((bf16[8,128,2,128]{3,1,2,0:T(8,128)(2,1)}), bf16[8,128,2,128]{3,1,2,0:T(8,128)(2,1)}, u32[]{:S(2)}, u32[]{:S(2)}) async-start(bf16[8,128,2,128]{3,1,2,0:T(8,128)(2,1)} %broadcast_in_dim.22), calls=%async_computation.3 | async-start | bytes 1048576 | tf_op jit(solution)/shard_map/all_to_all | solution.py:21
  128.9 18.6 %all-to-all-start.7 = ((f32[8,128,2,128]{3,1,2,0:T(8,128)}), f32[8,128,2,128]{3,1,2,0:T(8,128)}, u32[]{:S(2)}, u32[]{:S(2)}) async-start(f32[8,128,2,128]{3,1,2,0:T(8,128)} %bitcast.142), calls=%async_computation.7 | async-start | bytes 2097152 | tf_op jit(solution)/shard_map/all_to_all | solution.py:15
  147.5 18.2 %all-to-all-start.10 = ((f32[8,128,2,128]{3,1,2,0:T(8,128)}), f32[8,128,2,128]{3,1,2,0:T(8,128)}, u32[]{:S(2)}, u32[]{:S(2)}) async-start(f32[8,128,2,128]{3,1,2,0:T(8,128)} %bitcast.141), calls=%async_computation.10 | async-start | bytes 2097152 | tf_op jit(solution)/shard_map/all_to_all | solution.py:15
  165.8 16.6 %all-to-all-start.8 = ((bf16[128,2,128]{2,1,0:T(2,128)(2,1)}), bf16[128,2,128]{2,1,0:T(2,128)(2,1)}, u32[]{:S(2)}, u32[]{:S(2)}) async-start(bf16[128,2,128]{2,1,0:T(2,128)(2,1)} %copy.92), calls=%async_computation.8 | async-start | bytes 131072 | tf_op jit(solution)/shard_map/all_to_all | solution.py:78
  182.4 14.5 %all-to-all-start.11 = ((bf16[128,2,128]{2,1,0:T(2,128)(2,1)}), bf16[128,2,128]{2,1,0:T(2,128)(2,1)}, u32[]{:S(2)}, u32[]{:S(2)}) async-start(bf16[128,2,128]{2,1,0:T(2,128)(2,1)} %copy.97), calls=%async_computation.11 | async-start | bytes 131072 | tf_op jit(solution)/shard_map/all_to_all | solution.py:78
  198.7 13.3 %all-to-all-start.9 = ((bf16[8,4,64,128]{3,2,1,0:T(8,128)(2,1)}), bf16[8,4,64,128]{3,2,1,0:T(8,128)(2,1)}, u32[]{:S(2)}, u32[]{:S(2)}) async-start(bf16[8,4,64,128]{3,2,1,0:T(8,128)(2,1)} %broadcast_in_dim.26), calls=%async_computation.9 | async-start | bytes 1048576 | tf_op jit(solution)/shard_map/all_to_all | solution.py:21
  212.9 12.8 %all-to-all-start.12 = ((bf16[8,4,64,128]{3,2,1,0:T(8,128)(2,1)}), bf16[8,4,64,128]{3,2,1,0:T(8,128)(2,1)}, u32[]{:S(2)}, u32[]{:S(2)}) async-start(bf16[8,4,64,128]{3,2,1,0:T(8,128)(2,1)} %broadcast_in_dim.28), calls=%async_computation.12 | async-start | bytes 1048576 | tf_op jit(solution)/shard_map/all_to_all | solution.py:21
  221.5 18.1 %copy-start.1 = (bf16[1024,64]{0,1:T(8,128)(2,1)S(1)}, bf16[1024,64]{0,1:T(8,128)(2,1)}, u32[]{:S(2)}) copy-start(bf16[1024,64]{0,1:T(8,128)(2,1)} %param.7) | copy-start | bytes 393220
  225.7 8.8 %all-to-all-start.13 = ((f32[8,1,256]{2,1,0:T(1,128)}), f32[8,1,256]{2,1,0:T(1,128)S(1)}, u32[]{:S(2)}, u32[]{:S(2)}) async-start(f32[8,1,256]{2,1,0:T(1,128)} %reshape.65), calls=%async_computation.13 | async-start | bytes 16384 | tf_op jit(solution)/shard_map/all_to_all | solution.py:21
  229.4 257.3 %all-reduce.2.cloned.1.call-start = ((), (), s32[]{:S(2)}) async-start(), calls=%async_computation.14 | async-start | bytes 524288 | tf_op jit(solution)/shard_map/psum | solution.py:144
Sparse Core Ops, SparseCore 0:
  239.7 247.0 all-reduce.1
where the time goes:
time: 498 us; the launch traced here: 495 us
  waiting for transfers between devices  350 us (70%)
  starting transfers between devices  64.8 us (13%)
  matrix products  26.7 us (5%)
  local copies, waits for them, and re-layouts  19.7 us (4%)
  between operations  14.3 us (3%)
  blocking collectives  10.7 us (2%)
  other arithmetic  8.52 us (2%)
    psum x1, waiting for transfers between devices, on_device(): grad_router = lax.psum(local_router, ('dp', 'tensor'))  245 us
    all_to_all x4, waiting for transfers between devices, summed_on_arrival(): lax.all_to_all(blocks, axis, split_axis=0, concat_axis=0, tiled=True)  44.7 us
    all_to_all x5, waiting for transfers between devices, sent_to_all(): lax.all_to_all(jnp.broadcast_to(x[None], (length, *x.shape)), axis, 0, 0,...  27.3 us
    all_to_all x5, starting transfers between devices, sent_to_all(): lax.all_to_all(jnp.broadcast_to(x[None], (length, *x.shape)), axis, 0, 0,...  19.7 us
    all_to_all x2, waiting for transfers between devices, to_experts(): lax.all_to_all(shared_part, 'dp', split_axis=1, concat_axis=0, tiled=True)  18.9 us
    all_to_all x2, starting transfers between devices, to_experts(): lax.all_to_all(shared_part, 'dp', split_axis=1, concat_axis=0, tiled=True)  17.3 us
    all_to_all x4, starting transfers between devices, summed_on_arrival(): lax.all_to_all(blocks, axis, split_axis=0, concat_axis=0, tiled=True)  16.6 us
    all_to_all x2, waiting for transfers between devices, to_images(): lax.all_to_all(shared_part, 'dp', split_axis=0, concat_axis=1, tiled=True)  14.9 us
  transfers between devices with their start and end apart: 14, of which 14 were waited for; matrix products, arithmetic and copies ran while one was open for 7% of the time, Pallas kernels for 0%

commit v1 on v0

v1 whole, which is shorter than its diff:
```python
import jax
import jax.numpy as jnp
from jax import lax
from jax.sharding import PartitionSpec as P

WIDE = jnp.float32
LOW = jnp.bfloat16


def swapped(blocks, axis):
    return lax.all_to_all(blocks, axis, split_axis=0, concat_axis=0, tiled=True)


def sent_to_all(x, axis):
    return swapped(jnp.broadcast_to(x[None], (lax.axis_size(axis), *x.shape)), axis)


def to_blocks(x, parts):
    return jnp.moveaxis(x.reshape(*x.shape[:-1], parts, x.shape[-1] // parts), -2, 0)


def on_device(tokens, cotangent, dispatch_weight, w_in, w_out):
    tp = lax.axis_size("tensor")
    dp = lax.axis_size("dp")
    images, _, width = tokens.shape
    slots = dispatch_weight.shape[1]
    own = w_in.shape[0]
    part = width // tp
    logits = jnp.einsum("isd,de->ise", tokens, dispatch_weight, preferred_element_type=WIDE)
    local_max = jnp.max(logits, axis=1)
    weight = jnp.exp(logits - local_max[:, None, :])
    weight_low = weight.astype(LOW)
    combine = jax.nn.softmax(logits, axis=2)
    combine_low = combine.astype(LOW)
    rows = jnp.stack([
        jnp.einsum("ise,isd->ied", weight_low, tokens, preferred_element_type=WIDE),
        jnp.einsum("ise,isd->ied", combine_low, cotangent, preferred_element_type=WIDE),
    ]).astype(LOW)
    stats = sent_to_all(
        jnp.stack([local_max, jnp.sum(weight, axis=1), jnp.sum(weight_low.astype(WIDE), axis=1)]),
        "tensor",
    )
    top = jnp.max(stats[:, 0], axis=0)
    shrink = jnp.exp(stats[:, 0] - top)
    total = jnp.sum(stats[:, 1] * shrink, axis=0)
    total_low = jnp.sum(stats[:, 2] * shrink, axis=0)
    pieces = swapped(to_blocks(rows, tp), "tensor").astype(WIDE)
    slot_slice = jnp.sum(pieces[:, 0] * (shrink / total_low)[..., None], axis=0)
    grad_slice = jnp.sum(pieces[:, 1], axis=0)
    both = jnp.stack([slot_slice, grad_slice]).astype(LOW)
    both = both.reshape(2, images, dp, own, part).transpose(2, 0, 3, 1, 4)
    arrived = sent_to_all(swapped(both, "dp"), "tensor")
    full = arrived.transpose(2, 3, 1, 4, 0, 5).reshape(2, own, dp * images, width)
    slot_inputs, grad_slots_out = full[0], full[1]

    pre_act = jnp.einsum("eid,edf->eif", slot_inputs, w_in, preferred_element_type=WIDE)
    hidden_act, gelu_back = jax.vjp(jax.nn.gelu, pre_act)
    hidden_low = hidden_act.astype(LOW)
    out_part = jnp.einsum("eif,efd->eid", hidden_low, w_out, preferred_element_type=WIDE)
    grad_hidden = jnp.einsum("eid,efd->eif", grad_slots_out, w_out, preferred_element_type=WIDE)
    grad_pre = gelu_back(grad_hidden)[0].astype(LOW)
    in_part = jnp.einsum("eif,edf->eid", grad_pre, w_in, preferred_element_type=WIDE)
    grad_w_out = jnp.einsum(
        "eif,eid->efd", hidden_low, grad_slots_out, preferred_element_type=WIDE
    ).astype(LOW)
    grad_w_in = jnp.einsum(
        "eid,eif->edf", slot_inputs, grad_pre, preferred_element_type=WIDE
    ).astype(LOW)

    back = jnp.stack([out_part, in_part]).astype(LOW)
    back = back.reshape(2, own, dp, images, tp, part).transpose(4, 2, 0, 1, 3, 5)
    summed = jnp.sum(swapped(back, "tensor").astype(WIDE), axis=0).astype(LOW)
    home = swapped(summed, "dp")
    in_slice = home[:, 1].transpose(2, 0, 1, 3).reshape(images, slots, part).astype(WIDE)
    column_dot = jnp.sum(sent_to_all(jnp.sum(in_slice * slot_slice, axis=2), "tensor"), axis=0)
    gathered = sent_to_all(home, "tensor")
    gathered = gathered.transpose(2, 4, 1, 3, 0, 5).reshape(2, images, slots, width)
    slot_outputs, grad_slots_in = gathered[0], gathered[1]

    dispatch = weight * (jnp.exp(local_max - top) / total)[:, None, :]
    dispatch_low = dispatch.astype(LOW)
    grad_combine = jnp.einsum("isd,ied->ise", cotangent, slot_outputs, preferred_element_type=WIDE)
    grad_dispatch = jnp.einsum("isd,ied->ise", tokens, grad_slots_in, preferred_element_type=WIDE)
    row_dot = jnp.sum(grad_combine * combine, axis=2, keepdims=True)
    grad_logits = (
        combine * (grad_combine - row_dot) + dispatch * (grad_dispatch - column_dot[:, None, :])
    ).astype(LOW)
    local_router = jnp.einsum("isd,ise->de", tokens, grad_logits, preferred_element_type=WIDE)
    token_part = jnp.einsum(
        "ise,ied->isd", dispatch_low, grad_slots_in, preferred_element_type=WIDE
    )
    router_part = jnp.einsum(
        "ise,de->isd", grad_logits, dispatch_weight, preferred_element_type=WIDE
    )
    grad_tokens = (token_part + router_part).astype(LOW)

    over_tensor = jnp.sum(swapped(local_router.reshape(tp, part, slots), "tensor"), axis=0)
    over_dp = jnp.sum(swapped(over_tensor.reshape(dp, part // dp, slots), "dp"), axis=0)
    router_slice = sent_to_all(over_dp, "dp").reshape(part, slots)
    grad_router = sent_to_all(router_slice, "tensor").reshape(width, slots)
    return (grad_tokens, grad_router, grad_w_in, grad_w_out)


def solution(mesh):
    return jax.shard_map(
        on_device,
        mesh=mesh,
        in_specs=(
            P("dp", "tensor", None),
            P("dp", "tensor", None),
            P(),
            P("dp", None, "tensor"),
            P("dp", "tensor", None),
        ),
        out_specs=(P("dp", "tensor", None), P(), P("dp", None, "tensor"), P("dp", "tensor", None)),
        check_vma=False,
    )
```

time: 498 us -> 220 us (0.44)
  waiting for transfers between devices: 350 us -> 53 us
  blocking collectives: 10.7 us -> 73.5 us
  starting transfers between devices: 64.8 us -> 35.3 us
  between operations: 14.3 us -> 1.16 us
  matrix products: 26.7 us -> 21.2 us
  local copies, waits for them, and re-layouts: 19.7 us -> 24.9 us
    psum x1 -> x0, waiting for transfers between devices: 245 us -> none  [on_device(): grad_router = lax.psum(local_router, ('dp', 'tensor'))]
    all_to_all x1 -> x4, blocking collectives: 10.7 us -> 73.5 us  [swapped(): return lax.all_to_all(blocks, axis, split_axis=0, concat_axis=0, tiled=True)]
    all_to_all x13 -> x8, waiting for transfers between devices: 106 us -> 53 us  [swapped(): return lax.all_to_all(blocks, axis, split_axis=0, concat_axis=0, tiled=True)]
    all_to_all x13 -> x8, starting transfers between devices: 64.8 us -> 35.3 us  [swapped(): return lax.all_to_all(blocks, axis, split_axis=0, concat_axis=0, tiled=True)]
    slice x1 -> x7, local copies, waits for them, and re-layouts: 0.01 us -> 8.62 us  [the longest x3 4.78 us: on_device(): slot_outputs, grad_slots_in = (gathered[0], gathered[1])]
  transfers between devices with their start and end apart: 14 -> 8, of which waited for: 14 -> 7; matrix products, arithmetic and copies ran while one was open for 7% -> 9% of each run, Pallas kernels for 0% -> 0%
where the time goes in v1:
time: 220 us; the launch traced here: 218 us
  blocking collectives  73.5 us (33%)
  waiting for transfers between devices  53 us (24%)
  starting transfers between devices  35.3 us (16%)
  local copies, waits for them, and re-layouts  24.9 us (11%)
  matrix products  21.2 us (10%)
  other arithmetic  9.34 us (4%)
    all_to_all x4, blocking collectives, swapped(): return lax.all_to_all(blocks, axis, split_axis=0, concat_axis=0, tiled=True)  73.5 us
    all_to_all x8, waiting for transfers between devices, swapped(): return lax.all_to_all(blocks, axis, split_axis=0, concat_axis=0, tiled=True)  53 us
    all_to_all x8, starting transfers between devices, swapped(): return lax.all_to_all(blocks, axis, split_axis=0, concat_axis=0, tiled=True)  35.3 us
    unnamed x38, local copies, waits for them, and re-layouts  5.36 us
    slice x3, local copies, waits for them, and re-layouts, on_device(): slot_outputs, grad_slots_in = (gathered[0], gathered[1])  4.78 us
  transfers between devices with their start and end apart: 8, of which 7 were waited for; matrix products, arithmetic and copies ran while one was open for 9% of the time, Pallas kernels for 0%

profile of v1, /device:TPU:1, one launch (start us, length us, event | category | flops | bytes accessed | tf_op | source)
XLA Modules:
  0.0 218.3 jit_solution(613978100869677907)
XLA Ops:
  0.7 1.7 fusion.41
  3.4 5.9 %all-to-all-start = ((f32[8,1,768]{2,1,0:T(1,128)}), f32[8,1,768]{2,1,0:T(1,128)S(1)}, u32[]{:S(2)}, u32[]{:S(2)}) async-start(f32[8,1,768]{2,1,0:T(1,128)} %reshape.89), calls=%async_computation | async-start | bytes 49152 | tf_op jit(solution)/shard_map/all_to_all | solution.py:11
  9.9 1.4 convolution_convert_fusion.3
  15.0 5.1 %all-to-all-start.1 = ((bf16[8,2,4,64,128]{4,3,2,1,0:T(8,128)(2,1)}), bf16[8,2,4,64,128]{4,3,2,1,0:T(8,128)(2,1)S(1)}, u32[]{:S(2)}, u32[]{:S(2)}) async-start(bf16[8,2,4,64,128]{4,3,2,1,0:T(8,128)(2,1)} %maximum_bitcast_fusion), calls=%async_computation.1 | async-start | bytes 2097152 | tf_op jit(solution)/shard_map/all_to_all | solution.py:11
  22.1 12.7 %all-to-all-done.1 = bf16[8,2,4,64,128]{4,3,2,1,0:T(8,128)(2,1)S(1)} async-done(((bf16[8,2,4,64,128]{4,3,2,1,0:T(8,128)(2,1)}), bf16[8,2,4,64,128]{4,3,2,1,0:T(8,128)(2,1)S(1)}, u32[]{:S(2)}, u32[]{:S(2)}) %all-to-all-start.1) | async-done | bytes 1048608 | tf_op jit(solution)/shard_map/all_to_all | solution.py:11
  35.8 23.4 %all_to_all.60 = bf16[32,2,2,4,128]{4,2,3,1,0:T(2,128)(2,1)S(1)} all-to-all(bf16[32,2,2,4,128]{4,2,3,1,0:T(2,128)(2,1)S(1)} %copy.150), channel_id=1, replica_groups=mesh['dp'=32,'tensor'=8] {'dp'}, dimensions={0} | all-to-all | bytes 262144 | tf_op jit(solution)/shard_map/all_to_all | solution.py:11
  59.7 17.5 %all_to_all.61 = bf16[8,32,2,2,4,128]{5,4,1,3,2,0:T(4,128)(2,1)S(1)} all-to-all(bf16[8,32,2,2,4,128]{5,4,1,3,2,0:T(4,128)(2,1)S(1)} %broadcast_in_dim.17), channel_id=1, replica_groups=mesh['dp'=32,'tensor'=8] {'tensor'}, dimensions={0} | all-to-all | bytes 2097152 | tf_op jit(solution)/shard_map/all_to_all | solution.py:11
  77.2 1.3 fusion.39
  79.4 1.8 copy.152
  82.2 2.5 %fusion.42 = f32[2,128,512]{2,1,0:T(8,128)S(1)} fusion(bf16[2,128,1024]{2,1,0:T(8,128)(2,1)S(1)} %squeeze.32, bf16[2,512,1024]{2,1,0:T(8,128)(2,1)} %param.9), kind=kOutput, calls=%fused_computation.75 | convolution fusion | flops 268435456 | bytes 3145728 | tf_op jit(solution)/shard_map/eid,efd->eif/dot_general | solution.py:60
  89.1 16.6 %all_to_all.62 = bf16[8,32,2,2,4,128]{5,4,1,3,2,0:T(4,128)(2,1)S(1)} all-to-all(bf16[8,32,2,2,4,128]{5,4,1,3,2,0:T(4,128)(2,1)S(1)} %maximum_bitcast_fusion.1), channel_id=1, replica_groups=mesh['dp'=32,'tensor'=8] {'tensor'}, dimensions={0} | all-to-all | bytes 2097152 | tf_op jit(solution)/shard_map/all_to_all | solution.py:11
  106.4 16.0 %all_to_all.63 = bf16[32,2,2,4,128]{4,2,3,1,0:T(2,128)(2,1)S(1)} all-to-all(bf16[32,2,2,4,128]{4,2,3,1,0:T(2,128)(2,1)S(1)} %copy.157), channel_id=1, replica_groups=mesh['dp'=32,'tensor'=8] {'dp'}, dimensions={0} | all-to-all | bytes 262144 | tf_op jit(solution)/shard_map/all_to_all | solution.py:11
  123.4 3.3 %all-to-all-start.7 = ((f32[8,1,256]{2,1,0:T(1,128)}), f32[8,1,256]{2,1,0:T(1,128)S(1)}, u32[]{:S(2)}, u32[]{:S(2)}) async-start(f32[8,1,256]{2,1,0:T(1,128)} %reshape.91), calls=%async_computation.7 | async-start | bytes 16384 | tf_op jit(solution)/shard_map/all_to_all | solution.py:11
  126.9 4.9 %all-to-all-done.7 = f32[8,1,256]{2,1,0:T(1,128)S(1)} async-done(((f32[8,1,256]{2,1,0:T(1,128)}), f32[8,1,256]{2,1,0:T(1,128)S(1)}, u32[]{:S(2)}, u32[]{:S(2)}) %all-to-all-start.7) | async-done | bytes 8224 | tf_op jit(solution)/shard_map/all_to_all | solution.py:11
  131.7 2.0 broadcast_in_dim.18
  133.7 3.7 %all-to-all-start.6 = ((bf16[8,32,2,2,4,128]{5,3,1,4,2,0:T(2,128)(2,1)}), bf16[8,32,2,2,4,128]{5,3,1,4,2,0:T(2,128)(2,1)S(1)}, u32[]{:S(2)}, u32[]{:S(2)}) async-start(bf16[8,32,2,2,4,128]{5,3,1,4,2,0:T(2,128)(2,1)} %broadcast_in_dim.18), calls=%async_computation.6 | async-start | bytes 2097152 | tf_op jit(solution)/shard_map/all_to_all | solution.py:11
  138.3 14.1 %all-to-all-done.6 = bf16[8,32,2,2,4,128]{5,3,1,4,2,0:T(2,128)(2,1)S(1)} async-done(((bf16[8,32,2,2,4,128]{5,3,1,4,2,0:T(2,128)(2,1)}), bf16[8,32,2,2,4,128]{5,3,1,4,2,0:T(2,128)(2,1)S(1)}, u32[]{:S(2)}, u32[]{:S(2)}) %all-to-all-start.6) | async-done | bytes 1048608 | tf_op jit(solution)/shard_map/all_to_all | solution.py:11
  152.4 1.7 fusion.38
  155.7 1.6 convolution_bitcast_fusion.1
  157.3 2.5 %copy.159 = bf16[1,4,32,2,8,128]{5,4,3,2,1,0:T(8,128)(2,1)} copy(bf16[1,4,32,2,8,128]{5,3,2,1,0,4:T(2,128)(2,1)} %get-tuple-element.9) | data formatting | bytes 1048576 | tf_op jit(solution)/shard_map/slice | solution.py:78
  163.4 3.5 %all-to-all-start.8 = ((f32[8,128,64]{1,2,0:T(8,128)}), f32[8,128,64]{1,2,0:T(8,128)S(1)}, u32[]{:S(2)}, u32[]{:S(2)}) async-start(f32[8,128,64]{1,2,0:T(8,128)} %bitcast.149), calls=%async_computation.8 | async-start | bytes 524288 | tf_op jit(solution)/shard_map/all_to_all | solution.py:11
  167.0 3.3 %convolution_convert_fusion = bf16[2,512,1024]{2,1,0:T(8,128)(2,1)} fusion(bf16[2,128,1024]{2,1,0:T(8,128)(2,1)} %copy-done.3, f32[2,128,512]{2,1,0:T(8,128)} %copy-done.7), kind=kOutput, calls=%fused_computation.2 | convolution fusion | flops 270663680 | bytes 3145728 | tf_op jit(solution)/shard_map/eif,eid->efd/dot_general | solution.py:63
  170.2 2.4 %all-to-all-done.8 = f32[8,128,64]{1,2,0:T(8,128)S(1)} async-done(((f32[8,128,64]{1,2,0:T(8,128)}), f32[8,128,64]{1,2,0:T(8,128)S(1)}, u32[]{:S(2)}, u32[]{:S(2)}) %all-to-all-start.8) | async-done | bytes 262176 | tf_op jit(solution)/shard_map/all_to_all | solution.py:11
  174.9 6.3 %all-to-all-start.9 = ((f32[32,1,256]{2,1,0:T(1,128)}), f32[32,1,256]{2,1,0:T(1,128)S(1)}, u32[]{:S(2)}, u32[]{:S(2)}) async-start(f32[32,1,256]{2,1,0:T(1,128)} %reshape.93), calls=%async_computation.9 | async-start | bytes 65536 | tf_op jit(solution)/shard_map/all_to_all | solution.py:11
  181.3 3.0 %convolution_convert_fusion.1 = bf16[2,1024,512]{2,1,0:T(8,128)(2,1)} fusion(bf16[2,128,1024]{2,1,0:T(8,128)(2,1)S(1)} %copy-done.6, bf16[2,128,512]{2,1,0:T(8,128)(2,1)} %copy-done.8), kind=kOutput, calls=%fused_computation.3 | convolution fusion | flops 269484032 | bytes 2883584 | tf_op jit(solution)/shard_map/eid,eif->edf/dot_general | solution.py:66
  184.3 6.7 %all-to-all-done.9 = f32[32,1,256]{2,1,0:T(1,128)S(1)} async-done(((f32[32,1,256]{2,1,0:T(1,128)}), f32[32,1,256]{2,1,0:T(1,128)S(1)}, u32[]{:S(2)}, u32[]{:S(2)}) %all-to-all-start.9) | async-done | bytes 32800 | tf_op jit(solution)/shard_map/all_to_all | solution.py:11
  192.6 3.9 %all-to-all-start.10 = ((f32[32,1,256]{2,1,0:T(1,128)}), f32[32,1,256]{2,1,0:T(1,128)S(1)}, u32[]{:S(2)}, u32[]{:S(2)}) async-start(f32[32,1,256]{2,1,0:T(1,128)} %reshape.95), calls=%async_computation.10 | async-start | bytes 65536 | tf_op jit(solution)/shard_map/all_to_all | solution.py:11
  196.5 1.5 fusion.28
  198.0 8.3 %all-to-all-done.10 = f32[32,1,256]{2,1,0:T(1,128)S(1)} async-done(((f32[32,1,256]{2,1,0:T(1,128)}), f32[32,1,256]{2,1,0:T(1,128)S(1)}, u32[]{:S(2)}, u32[]{:S(2)}) %all-to-all-start.10) | async-done | bytes 32800 | tf_op jit(solution)/shard_map/all_to_all | solution.py:11
  207.9 3.4 %all-to-all-start.11 = ((f32[8,128,64]{1,2,0:T(8,128)}), f32[8,128,64]{1,2,0:T(8,128)S(1)}, u32[]{:S(2)}, u32[]{:S(2)}) async-start(f32[8,128,64]{1,2,0:T(8,128)} %broadcast_in_dim.23), calls=%async_computation.11 | async-start | bytes 524288 | tf_op jit(solution)/shard_map/all_to_all | solution.py:11
  211.3 2.4 %fusion.2 = bf16[4,72,1024]{2,1,0:T(8,128)(2,1)} fusion(f32[4,72,1024]{2,1,0:T(8,128)} %fusion.28, bf16[4,72,64]{1,2,0:T(8,128)(2,1)S(1)} %copy-done.10, bf16[1024,64]{0,1:T(8,128)(2,1)S(1)} %copy-done.11), kind=kOutput, calls=%fused_computation.5 | convolution fusion | flops 38338560 | bytes 1937408 | tf_op jit(solution)/shard_map/ise,de->isd/dot_general | solution.py:92
  213.7 3.9 %all-to-all-done.11 = f32[8,128,64]{1,2,0:T(8,128)S(1)} async-done(((f32[8,128,64]{1,2,0:T(8,128)}), f32[8,128,64]{1,2,0:T(8,128)S(1)}, u32[]{:S(2)}, u32[]{:S(2)}) %all-to-all-start.11) | async-done | bytes 262176 | tf_op jit(solution)/shard_map/all_to_all | solution.py:11
  (96 shorter events, 28.8 us)
Async XLA Ops:
  0.6 84.1 %copy-start = (bf16[2,1024,512]{2,1,0:T(8,128)(2,1)S(1)}, bf16[2,1024,512]{2,1,0:T(8,128)(2,1)}, u32[]{:S(2)}) copy-start(bf16[2,1024,512]{2,1,0:T(8,128)(2,1)} %param.8) | copy-start | bytes 6291460
  0.6 10.7 %copy-start.4 = (bf16[4,72,1024]{2,1,0:T(8,128)(2,1)S(1)}, bf16[4,72,1024]{2,1,0:T(8,128)(2,1)}, u32[]{:S(2)}) copy-start(bf16[4,72,1024]{2,1,0:T(8,128)(2,1)} %param.6) | copy-start | bytes 1769476
  3.4 11.7 %all-to-all-start = ((f32[8,1,768]{2,1,0:T(1,128)}), f32[8,1,768]{2,1,0:T(1,128)S(1)}, u32[]{:S(2)}, u32[]{:S(2)}) async-start(f32[8,1,768]{2,1,0:T(1,128)} %reshape.89), calls=%async_computation | async-start | bytes 49152 | tf_op jit(solution)/shard_map/all_to_all | solution.py:11
  15.0 19.8 %all-to-all-start.1 = ((bf16[8,2,4,64,128]{4,3,2,1,0:T(8,128)(2,1)}), bf16[8,2,4,64,128]{4,3,2,1,0:T(8,128)(2,1)S(1)}, u32[]{:S(2)}, u32[]{:S(2)}) async-start(bf16[8,2,4,64,128]{4,3,2,1,0:T(8,128)(2,1)} %maximum_bitcast_fusion), calls=%async_computation.1 | async-start | bytes 2097152 | tf_op jit(solution)/shard_map/all_to_all | solution.py:11
  79.4 5.4 %copy-start.3 = (bf16[2,128,1024]{2,1,0:T(8,128)(2,1)}, bf16[2,128,1024]{2,1,0:T(8,128)(2,1)S(1)}, u32[]{:S(2)}) copy-start(bf16[2,128,1024]{2,1,0:T(8,128)(2,1)S(1)} %squeeze.32) | copy-start | bytes 1572868
  82.2 2.5 %copy-start.5 = (bf16[2,128,1024]{2,1,0:T(8,128)(2,1)S(1)}, bf16[2,128,1024]{2,1,0:T(8,128)(2,1)}, u32[]{:S(2)}) copy-start(bf16[2,128,1024]{2,1,0:T(8,128)(2,1)} %squeeze.31) | copy-start | bytes 1572868
  85.5 1.2 copy-start.8
  85.5 1.2 copy-start.7
  85.5 1.9 copy-start.2
  106.4 31.1 %copy-start.12 = (f32[4,64]{1,0:T(4,128)S(1)}, f32[4,64]{1,0:T(4,128)}, u32[]{:S(2)}) copy-start(f32[4,64]{1,0:T(4,128)} %get-tuple-element.6) | copy-start | bytes 3076
  123.4 8.3 %all-to-all-start.7 = ((f32[8,1,256]{2,1,0:T(1,128)}), f32[8,1,256]{2,1,0:T(1,128)S(1)}, u32[]{:S(2)}, u32[]{:S(2)}) async-start(f32[8,1,256]{2,1,0:T(1,128)} %reshape.91), calls=%async_computation.7 | async-start | bytes 16384 | tf_op jit(solution)/shard_map/all_to_all | solution.py:11
  133.7 18.6 %all-to-all-start.6 = ((bf16[8,32,2,2,4,128]{5,3,1,4,2,0:T(2,128)(2,1)}), bf16[8,32,2,2,4,128]{5,3,1,4,2,0:T(2,128)(2,1)S(1)}, u32[]{:S(2)}, u32[]{:S(2)}) async-start(bf16[8,32,2,2,4,128]{5,3,1,4,2,0:T(2,128)(2,1)} %broadcast_in_dim.18), calls=%async_computation.6 | async-start | bytes 2097152 | tf_op jit(solution)/shard_map/all_to_all | solution.py:11
  155.7 6.3 %copy-start.1 = (bf16[4,72,1024]{2,1,0:T(8,128)(2,1)S(1)}, bf16[4,72,1024]{2,1,0:T(8,128)(2,1)}, u32[]{:S(2)}) copy-start(bf16[4,72,1024]{2,1,0:T(8,128)(2,1)} %param.5) | copy-start | bytes 1769476
  162.4 1.0 copy-start.9
  163.4 17.8 %copy-start.6 = (bf16[2,128,1024]{2,1,0:T(8,128)(2,1)S(1)}, bf16[2,128,1024]{2,1,0:T(8,128)(2,1)}, u32[]{:S(2)}) copy-start(bf16[2,128,1024]{2,1,0:T(8,128)(2,1)} %squeeze.31) | copy-start | bytes 1572868
  163.4 9.3 %all-to-all-start.8 = ((f32[8,128,64]{1,2,0:T(8,128)}), f32[8,128,64]{1,2,0:T(8,128)S(1)}, u32[]{:S(2)}, u32[]{:S(2)}) async-start(f32[8,128,64]{1,2,0:T(8,128)} %bitcast.149), calls=%async_computation.8 | async-start | bytes 524288 | tf_op jit(solution)/shard_map/all_to_all | solution.py:11
  174.9 16.1 %all-to-all-start.9 = ((f32[32,1,256]{2,1,0:T(1,128)}), f32[32,1,256]{2,1,0:T(1,128)S(1)}, u32[]{:S(2)}, u32[]{:S(2)}) async-start(f32[32,1,256]{2,1,0:T(1,128)} %reshape.93), calls=%async_computation.9 | async-start | bytes 65536 | tf_op jit(solution)/shard_map/all_to_all | solution.py:11
  184.3 27.0 %copy-start.10 = (bf16[4,72,64]{1,2,0:T(8,128)(2,1)S(1)}, bf16[4,72,64]{1,2,0:T(8,128)(2,1)}, u32[]{:S(2)}) copy-start(bf16[4,72,64]{1,2,0:T(8,128)(2,1)} %copy-done.9) | copy-start | bytes 110596
  184.3 27.0 %copy-start.11 = (bf16[1024,64]{0,1:T(8,128)(2,1)S(1)}, bf16[1024,64]{0,1:T(8,128)(2,1)}, u32[]{:S(2)}) copy-start(bf16[1024,64]{0,1:T(8,128)(2,1)} %param.7) | copy-start | bytes 393220
  192.6 13.7 %all-to-all-start.10 = ((f32[32,1,256]{2,1,0:T(1,128)}), f32[32,1,256]{2,1,0:T(1,128)S(1)}, u32[]{:S(2)}, u32[]{:S(2)}) async-start(f32[32,1,256]{2,1,0:T(1,128)} %reshape.95), calls=%async_computation.10 | async-start | bytes 65536 | tf_op jit(solution)/shard_map/all_to_all | solution.py:11
  207.9 9.7 %all-to-all-start.11 = ((f32[8,128,64]{1,2,0:T(8,128)}), f32[8,128,64]{1,2,0:T(8,128)S(1)}, u32[]{:S(2)}, u32[]{:S(2)}) async-start(f32[8,128,64]{1,2,0:T(8,128)} %broadcast_in_dim.23), calls=%async_computation.11 | async-start | bytes 524288 | tf_op jit(solution)/shard_map/all_to_all | solution.py:11

commit v2 on v1

v2 whole, which is shorter than its diff:
```python
import functools
import math

import jax
import jax.numpy as jnp
from jax import lax
from jax.experimental import pallas as pl
from jax.experimental.pallas import tpu as pltpu
from jax.sharding import PartitionSpec as P

WIDE = jnp.float32
LOW = jnp.bfloat16
MESH = pl.DeviceIdType.MESH
LANES = 128
LEAST = -3.0e38


def dot(a, b, over):
    return lax.dot_general(a, b, (over, ((), ())), preferred_element_type=WIDE)


def plain(a, b):
    return dot(a, b, ((1,), (0,)))


def rows_by_rows(a, b):
    return dot(a, b, ((1,), (1,)))


def columns_by_columns(a, b):
    return dot(a, b, ((0,), (0,)))


def iotas(shape):
    return lax.broadcasted_iota(jnp.int32, shape, 0), lax.broadcasted_iota(jnp.int32, shape, 1)


def kernel(
    tp, dp, images, own,
    tok, cot, router, w_in_hbm, w_out_hbm,
    grad_tok, grad_router, grad_in_hbm, grad_out_hbm,
    w_in, w_out, grad_in, grad_out, spread, weight, combine, dispatch, slot_slice,
    send_rows, recv_rows, send_slots, recv_slots, full, flat, sorted_rows, stats, stats_in,
    dots, dots_in, part, part_in, piece, piece_in, whole,
    local_sem, t_send, t_recv, d_send, d_recv,
):
    me_t, me_d = lax.axis_index("tensor"), lax.axis_index("dp")
    n = tok.shape[0]
    group = own * images
    c = dp * group
    seq = n // images
    slots = dp * own
    half = c // own

    def copy_tensor(phase, k, src, dst, slot):
        to = lax.rem(me_t + k, tp)
        return pltpu.make_async_remote_copy(
            src_ref=src(to), dst_ref=dst(slot),
            send_sem=t_send.at[phase, k], recv_sem=t_recv.at[phase, k],
            device_id={"tensor": to}, device_id_type=MESH,
        )

    def start_tensor(phase, src, dst):
        for k in range(1, tp):
            copy_tensor(phase, k, src, dst, me_t).start()

    def await_tensor(phase, src, dst):
        for k in range(1, tp):
            copy_tensor(phase, k, src, dst, lax.rem(me_t + tp - k, tp)).wait_recv()

    def drain_tensor(phase, src, dst):
        for k in range(1, tp):
            copy_tensor(phase, k, src, dst, me_t).wait_send()

    def start_dp(phase, src, dst):
        def one(k, carry):
            to = lax.rem(me_d + k, dp)
            pltpu.make_async_remote_copy(
                src_ref=src(to), dst_ref=dst(me_d),
                send_sem=d_send.at[phase], recv_sem=d_recv.at[phase],
                device_id={"dp": to}, device_id_type=MESH,
            ).start()
            return carry
        lax.fori_loop(1, dp, one, 0)

    def all_dp(phase, out, into):
        return pltpu.make_async_remote_copy(
            src_ref=out.at[pl.ds(0, dp - 1)], dst_ref=into.at[pl.ds(0, dp - 1)],
            send_sem=d_send.at[phase], recv_sem=d_recv.at[phase],
            device_id={"dp": lax.rem(me_d + 1, dp)}, device_id_type=MESH,
        )

    STATS, DOTS, PART, WHOLE = 8, 9, 10, 11
    rows_of = [
        (lot, lambda to, lot=lot: send_rows.at[lot, to], lambda s, lot=lot: recv_rows.at[lot, s])
        for lot in range(4)
    ]
    slots_of = [
        (4 + lot, lambda to, lot=lot: recv_slots.at[lot], lambda s, lot=lot: full.at[lot, s])
        for lot in range(4)
    ]
    stats_of = (STATS, lambda to: stats, lambda s: stats_in.at[s])
    dots_of = (DOTS, lambda to: dots, lambda s: dots_in.at[s])
    part_of = (PART, lambda to: part.at[to], lambda s: part_in.at[s])
    whole_of = (WHOLE, lambda to: whole.at[me_t], lambda s: whole.at[s])

    loads = [
        pltpu.make_async_copy(w_in_hbm, w_in, local_sem.at[0]),
        pltpu.make_async_copy(w_out_hbm, w_out, local_sem.at[1]),
    ]
    for load in loads:
        load.start()

    barrier = pltpu.get_barrier_semaphore()

    def greet(axis, me, size):
        def one(k, carry):
            pl.semaphore_signal(
                barrier, inc=1, device_id={axis: lax.rem(me + k, size)}, device_id_type=MESH
            )
            return carry
        lax.fori_loop(1, size, one, 0)

    greet("tensor", me_t, tp)
    greet("dp", me_d, dp)

    row, col = iotas((c, slots))
    choose = jnp.where((row >= col * images) & (row < col * images + images), 1.0, 0.0).astype(LOW)
    spread[...] = rows_by_rows(choose, router[...]).astype(LOW)
    row, col = iotas((c, n))
    begin = lax.rem(row, images) * seq
    ours = (col >= begin) & (col < begin + seq)
    masked = jnp.where(ours, rows_by_rows(spread[...], tok[...]), LEAST)
    top = jnp.max(masked, axis=1, keepdims=True)
    exponent = jnp.where(ours, jnp.exp(masked - top), 0.0)
    exponent_low = exponent.astype(LOW)
    weight[...] = exponent
    lane = iotas((c, LANES))[1]
    packed = jnp.where(
        lane == 0, top,
        jnp.where(
            lane == 1, jnp.sum(exponent, axis=1, keepdims=True),
            jnp.sum(exponent_low.astype(WIDE), axis=1, keepdims=True),
        ),
    )
    stats[...] = jnp.transpose(packed)[0:8, :]

    def cut(rows, lot):
        for t in range(tp):
            block = rows[:, t * LANES:(t + 1) * LANES].reshape(dp, group, LANES)
            send_rows[lot, t] = block.astype(LOW)

    cut(plain(exponent_low, tok[...]), 0)
    pl.semaphore_wait(barrier, tp + dp - 2)
    start_tensor(*stats_of)
    start_tensor(*rows_of[0])

    best = jnp.max(masked, axis=0, keepdims=True)
    raised = jnp.where(ours, jnp.exp(masked - best), 0.0)
    share = raised / jnp.sum(raised, axis=0, keepdims=True)
    combine[...] = share
    cut(plain(share.astype(LOW), cot[...]), 1)
    start_tensor(*rows_of[1])

    await_tensor(*stats_of)
    stats_in[me_t] = stats[...]
    most = stats_in[0, 0:1]
    for s in range(1, tp):
        most = jnp.maximum(most, stats_in[s, 0:1])
    shrinks = [jnp.exp(stats_in[s, 0:1] - most) for s in range(tp)]
    total = sum(stats_in[s, 1:2] * shrinks[s] for s in range(tp))
    total_low = sum(stats_in[s, 2:3] * shrinks[s] for s in range(tp))
    lines = [shrink / total_low for shrink in shrinks]
    lines.append(jnp.exp(stats[0:1] - most) / total)
    line_row = iotas((LANES, c))[0]
    table = jnp.zeros((LANES, c), WIDE)
    for s, line in enumerate(lines):
        table = jnp.where(line_row == s, line, table)
    table = jnp.transpose(table)
    dispatch[...] = weight[...] * table[:, tp:tp + 1]

    def summed(lot, scales=None):
        await_tensor(*rows_of[lot])
        recv_rows[lot, me_t] = send_rows[lot, me_t]
        total_rows = None
        for s in range(tp):
            term = recv_rows[lot, s].astype(WIDE).reshape(c, LANES)
            if scales is not None:
                term = term * scales[:, s:s + 1]
            total_rows = term if total_rows is None else total_rows + term
        return total_rows

    def pass_on(total_rows, lot):
        send_slots[lot] = total_rows.reshape(dp, group, LANES).astype(LOW)
        start_dp(lot, lambda to: send_slots.at[lot, to], lambda s: recv_slots.at[lot, s])

    def gather(lot):
        all_dp(lot, send_slots.at[lot], recv_slots.at[lot]).wait_recv()
        recv_slots[lot, me_d] = send_slots[lot, me_d]
        start_tensor(*slots_of[lot])

    def assembled(lot):
        await_tensor(*slots_of[lot])
        full[lot, me_t] = recv_slots[lot]
        for t in range(tp):
            block = full[lot, t].astype(WIDE).reshape(c, LANES)
            flat[lot, :, t * LANES:(t + 1) * LANES] = block.astype(LOW)
        return flat[lot]

    slot_slice[...] = summed(0, table)
    pass_on(slot_slice[...], 0)
    pass_on(summed(1), 1)
    gather(0)
    gather(1)

    def matching(q, other):
        late = (q >= half).astype(jnp.int32)
        image = lax.rem(q, images)
        return other == own * (q - late * half - image) + image + late * images

    row, col = iotas((c, c))
    sort = jnp.where(matching(row, col), 1.0, 0.0).astype(LOW)
    unsort = jnp.where(matching(col, row), 1.0, 0.0).astype(LOW)
    for load in loads:
        load.wait()
    root = math.sqrt(2.0 / math.pi)
    sorted_rows[0] = plain(sort, assembled(0)).astype(LOW)
    hidden, slope, results = [], [], []
    for e in range(own):
        pre = plain(sorted_rows[0, e * half:(e + 1) * half], w_in[e])
        square = pre * pre
        bent = jnp.tanh(root * (pre + 0.044715 * (square * pre)))
        hidden.append((0.5 * pre * (1.0 + bent)).astype(LOW))
        slope.append(
            0.5 * (1.0 + bent)
            + 0.5 * pre * (1.0 - bent * bent) * (root * (1.0 + 3.0 * 0.044715 * square))
        )
        results.append(plain(hidden[e], w_out[e]).astype(LOW))
    cut(plain(unsort, jnp.concatenate(results)), 2)
    start_tensor(*rows_of[2])
    sorted_rows[1] = plain(sort, assembled(1)).astype(LOW)
    grad_pre, results = [], []
    for e in range(own):
        grad_hidden = rows_by_rows(sorted_rows[1, e * half:(e + 1) * half], w_out[e])
        grad_pre.append((slope[e] * grad_hidden).astype(LOW))
        results.append(rows_by_rows(grad_pre[e], w_in[e]).astype(LOW))
    cut(plain(unsort, jnp.concatenate(results)), 3)
    start_tensor(*rows_of[3])
    for e in range(own):
        here = slice(e * half, (e + 1) * half)
        grad_out[e] = columns_by_columns(hidden[e], sorted_rows[1, here]).astype(LOW)
        grad_in[e] = columns_by_columns(sorted_rows[0, here], grad_pre[e]).astype(LOW)
    stores = [
        pltpu.make_async_copy(grad_in, grad_in_hbm, local_sem.at[2]),
        pltpu.make_async_copy(grad_out, grad_out_hbm, local_sem.at[3]),
    ]
    for store in stores:
        store.start()

    pass_on(summed(2), 2)
    pass_on(summed(3), 3)
    gather(2)
    gather(3)
    products = recv_slots[3].astype(WIDE).reshape(c, LANES) * slot_slice[...]
    own_dots = jnp.broadcast_to(jnp.sum(products, axis=1, keepdims=True), (c, LANES))
    dots[...] = jnp.transpose(own_dots)[0:8, :]
    start_tensor(*dots_of)

    slot_out = assembled(2)
    share = combine[...]
    grad_share = rows_by_rows(slot_out, cot[...])
    row_dot = jnp.sum(grad_share * share, axis=0, keepdims=True)
    from_share = share * (grad_share - row_dot)
    slot_grad = assembled(3)
    grad_weight = rows_by_rows(slot_grad, tok[...])
    await_tensor(*dots_of)
    dots_in[me_t] = dots[...]
    dot_line = dots_in[0, 0:1]
    for s in range(1, tp):
        dot_line = dot_line + dots_in[s, 0:1]
    column_dot = jnp.transpose(jnp.broadcast_to(dot_line, (LANES, c)))[:, 0:1]
    spots = dispatch[...]
    grad_logits = (from_share + spots * (grad_weight - column_dot)).astype(LOW)
    row, col = iotas((slots, c))
    fold = jnp.where((col >= row * images) & (col < row * images + images), 1.0, 0.0).astype(LOW)
    by_slot = plain(fold, grad_logits).astype(LOW)
    local_router = plain(by_slot, tok[...])
    for t in range(tp):
        part[t] = local_router[:, t * LANES:(t + 1) * LANES]
    start_tensor(*part_of)
    grad_tok[...] = (
        columns_by_columns(spots.astype(LOW), slot_grad)
        + columns_by_columns(grad_logits, spread[...])
    ).astype(LOW)

    await_tensor(*part_of)
    part_in[me_t] = part[me_t]
    router_rows = part_in[0]
    for s in range(1, tp):
        router_rows = router_rows + part_in[s]
    high = slots // dp
    for k in range(dp):
        piece[k] = router_rows[k * high:(k + 1) * high]
    start_dp(4, lambda to: piece.at[to], lambda s: piece_in.at[s])
    all_dp(4, piece, piece_in).wait_recv()
    piece_in[me_d] = piece[me_d]
    whole[me_t, me_d] = jnp.sum(piece_in[...], axis=0)
    start_dp(5, lambda to: whole.at[me_t, me_d], lambda s: whole.at[me_t, s])
    all_dp(5, whole.at[me_t], whole.at[me_t]).wait_recv()
    start_tensor(*whole_of)
    await_tensor(*whole_of)
    for t in range(tp):
        for k in range(dp):
            grad_router[k * high:(k + 1) * high, t * LANES:(t + 1) * LANES] = whole[t, k]

    for phase in [*rows_of, *slots_of, stats_of, dots_of, part_of, whole_of]:
        drain_tensor(*phase)
    for lot in range(4):
        all_dp(lot, send_slots.at[lot], recv_slots.at[lot]).wait_send()
    all_dp(4, piece, piece_in).wait_send()
    all_dp(5, whole.at[me_t], whole.at[me_t]).wait_send()
    for store in stores:
        store.wait()


def on_device(tokens, cotangent, dispatch_weight, w_in, w_out):
    tp, dp = lax.axis_size("tensor"), lax.axis_size("dp")
    images, seq, width = tokens.shape
    own, _, inner = w_in.shape
    n, slots, group = images * seq, dp * own, own * images
    c = dp * group
    vmem = pltpu.VMEM
    outs = pl.pallas_call(
        functools.partial(kernel, tp, dp, images, own),
        name="moe_back",
        out_shape=(
            jax.ShapeDtypeStruct((n, width), LOW),
            jax.ShapeDtypeStruct((slots, width), WIDE),
            jax.ShapeDtypeStruct(w_in.shape, LOW),
            jax.ShapeDtypeStruct(w_out.shape, LOW),
        ),
        in_specs=[pl.BlockSpec(memory_space=pltpu.VMEM)] * 3
        + [pl.BlockSpec(memory_space=pl.ANY)] * 2,
        out_specs=tuple(
            [pl.BlockSpec(memory_space=pltpu.VMEM)] * 2 + [pl.BlockSpec(memory_space=pl.ANY)] * 2
        ),
        scratch_shapes=[
            vmem(w_in.shape, LOW), vmem(w_out.shape, LOW),
            vmem(w_in.shape, LOW), vmem(w_out.shape, LOW),
            vmem((c, width), LOW),
            vmem((c, n), WIDE), vmem((c, n), WIDE), vmem((c, n), WIDE),
            vmem((c, LANES), WIDE),
            vmem((4, tp, dp, group, LANES), LOW), vmem((4, tp, dp, group, LANES), LOW),
            vmem((4, dp, group, LANES), LOW), vmem((4, dp, group, LANES), LOW),
            vmem((4, tp, dp, group, LANES), LOW),
            vmem((4, c, width), LOW), vmem((2, c, width), LOW),
            vmem((8, c), WIDE), vmem((tp, 8, c), WIDE),
            vmem((8, c), WIDE), vmem((tp, 8, c), WIDE),
            vmem((tp, slots, LANES), WIDE), vmem((tp, slots, LANES), WIDE),
            vmem((dp, slots // dp, LANES), WIDE), vmem((dp, slots // dp, LANES), WIDE),
            vmem((tp, dp, slots // dp, LANES), WIDE),
            pltpu.SemaphoreType.DMA((4,)),
            pltpu.SemaphoreType.DMA((12, tp)), pltpu.SemaphoreType.DMA((12, tp)),
            pltpu.SemaphoreType.DMA((6,)), pltpu.SemaphoreType.DMA((6,)),
        ],
        compiler_params=pltpu.CompilerParams(
            collective_id=0, has_side_effects=True, vmem_limit_bytes=60 * 2**20
        ),
    )(
        tokens.reshape(n, width), cotangent.reshape(n, width), dispatch_weight, w_in, w_out
    )
    grad_tokens, grad_router, grad_w_in, grad_w_out = outs
    return (grad_tokens.reshape(tokens.shape), grad_router.T, grad_w_in, grad_w_out)


def solution(mesh):
    return jax.shard_map(
        on_device,
        mesh=mesh,
        in_specs=(
            P("dp", "tensor", None),
            P("dp", "tensor", None),
            P(),
            P("dp", None, "tensor"),
            P("dp", "tensor", None),
        ),
        out_specs=(P("dp", "tensor", None), P(), P("dp", None, "tensor"), P("dp", "tensor", None)),
        check_vma=False,
    )
```

time: 220 us -> 111 us (0.50)
  Pallas kernels: 0 us -> 100 us
  blocking collectives: 73.5 us -> 0 us
  waiting for transfers between devices: 53 us -> 0 us
  starting transfers between devices: 35.3 us -> 0 us
  matrix products: 21.2 us -> 0 us
  local copies, waits for them, and re-layouts: 24.9 us -> 9.85 us
  other arithmetic: 9.34 us -> 0 us
    pallas_call x0 -> x1, Pallas kernels: none -> 100 us  [on_device(): pl.pallas_call(functools.partial(kernel, tp, dp, images, own), name='moe_...]
    all_to_all x4 -> x0, blocking collectives: 73.5 us -> none  [swapped(): return lax.all_to_all(blocks, axis, split_axis=0, concat_axis=0, tiled=True)]
    all_to_all x8 -> x0, waiting for transfers between devices: 53 us -> none  [swapped(): return lax.all_to_all(blocks, axis, split_axis=0, concat_axis=0, tiled=True)]
    all_to_all x8 -> x0, starting transfers between devices: 35.3 us -> none  [swapped(): return lax.all_to_all(blocks, axis, split_axis=0, concat_axis=0, tiled=True)]
    dot_general x14 -> x0, matrix products: 21.2 us -> none  [the longest x1 3.28 us: on_device(): jnp.einsum('eif,eid->efd', hidden_low, grad_slots_out, preferred_element_...]
    slice x7 -> x0, local copies, waits for them, and re-layouts: 8.62 us -> none  [the longest x3 4.78 us: on_device(): slot_outputs, grad_slots_in = (gathered[0], gathered[1])]
    unnamed x38 -> x7, local copies, waits for them, and re-layouts: 5.36 us -> 9.85 us
    squeeze x4 -> x0, local copies, waits for them, and re-layouts: 3.52 us -> none  [the longest x2 2.28 us: on_device(): slot_outputs, grad_slots_in = (gathered[0], gathered[1])]
  transfers between devices with their start and end apart: 8 -> 0, of which waited for: 7 -> 0; matrix products, arithmetic and copies ran while one was open for 9% -> 0% of each run, Pallas kernels for 0% -> 0%
where the time goes in v2:
time: 111 us
  Pallas kernels  100 us (90%)
  local copies, waits for them, and re-layouts  9.85 us (9%)
    pallas_call x1, Pallas kernels, on_device(): pl.pallas_call(functools.partial(kernel, tp, dp, images, own), name='moe_...  100 us
    unnamed x7, local copies, waits for them, and re-layouts  9.85 us

profile of v2, /device:TPU:1, one launch (start us, length us, event | category | flops | bytes accessed | tf_op | source)
XLA Modules:
  0.0 110.8 jit_solution(1960352651774508207)
XLA Ops:
  0.6 1.7 %copy.9.router = bf16[1024,64]{1,0:T(8,128)(2,1)} copy(bf16[1024,64]{0,1:T(8,128)(2,1)} %param.7) | data formatting | bytes 262144 | tf_op args[2]
  2.4 100.3 %moe_back.1 = (bf16[288,1024]{1,0:T(8,128)(2,1)}, f32[64,1024]{1,0:T(8,128)}, bf16[2,1024,512]{2,1,0:T(8,128)(2,1)}, bf16[2,512,1024]{2,1,0:T(8,128)(2,1)}) custom-call(bf16[288,1024]{1,0:T(8,128)(2,1)} %bitcast.5, bf16[288,1024]{1,0:T(8,128)(2,1)} %bitcast.6, bf16[1024,64]{1,0:T(8,128)(2,1)} %copy.9.router, bf16[2,1024,512]{2,1,0:T(8,128)(2,1)} %w_in_hbm.1, ...), custom_call_target="tpu_custom_call" | custom-call | tf_op jit(solution)/shard_map/moe_back/pallas_call | solution.py:333
  102.7 1.9 %copy.14 = bf16[4,72,1024]{2,1,0:T(8,128)(2,1)} copy(bf16[4,72,1024]{2,1,0:T(8,128)(2,1)} %bitcast.4) | data formatting | bytes 1179648
  104.6 1.7 %copy.15 = f32[1024,64]{0,1:T(8,128)} copy(f32[1024,64]{0,1:T(8,128)} %bitcast.7) | data formatting | bytes 524288
  106.3 0.0 copy-start
  106.3 3.2 %copy.16 = bf16[2,1024,512]{2,1,0:T(8,128)(2,1)} copy(bf16[2,1024,512]{2,1,0:T(8,128)(2,1)} %get-tuple-element.18) | data formatting | bytes 4194304
  109.5 0.0 copy-done
  109.5 1.3 %copy.17 = bf16[2,512,1024]{2,1,0:T(8,128)(2,1)} copy(bf16[2,512,1024]{2,1,0:T(8,128)(2,1)S(1)} %copy-done) | data formatting | bytes 4194304
Async XLA Ops:
  106.3 3.2 %copy-start = (bf16[2,512,1024]{2,1,0:T(8,128)(2,1)S(1)}, bf16[2,512,1024]{2,1,0:T(8,128)(2,1)}, u32[]{:S(2)}) copy-start(bf16[2,512,1024]{2,1,0:T(8,128)(2,1)} %get-tuple-element.19) | copy-start | bytes 6291460

commit v3 on v2

--- a/solution.py
+++ b/solution.py
@@ -13,6 +13,7 @@
 MESH = pl.DeviceIdType.MESH
 LANES = 128
 LEAST = -3.0e38
+PLANE = 4
 
 
 def dot(a, b, over):
@@ -37,12 +38,12 @@
 
 def kernel(
     tp, dp, images, own,
-    tok, cot, router, w_in_hbm, w_out_hbm,
-    grad_tok, grad_router, grad_in_hbm, grad_out_hbm,
-    w_in, w_out, grad_in, grad_out, spread, weight, combine, dispatch, slot_slice,
+    tok_hbm, cot_hbm, router, w_in_hbm, w_out_hbm,
+    grad_tok, grad_router, grad_in, grad_out,
+    tok, cot, w_in, w_out, spread, weight, combine, dispatch, slot_slice,
     send_rows, recv_rows, send_slots, recv_slots, full, flat, sorted_rows, stats, stats_in,
-    dots, dots_in, part, part_in, piece, piece_in, whole,
-    local_sem, t_send, t_recv, d_send, d_recv,
+    dots, dots_in, part, part_in, piece, piece_in, whole, final,
+    local_sem, t_send, t_recv, d_send, d_recv, z_send, z_recv,
 ):
     me_t, me_d = lax.axis_index("tensor"), lax.axis_index("dp")
     n = tok.shape[0]
@@ -51,6 +52,9 @@
     seq = n // images
     slots = dp * own
     half = c // own
+    members, depth = PLANE * tp, dp // PLANE
+    me_z, me_q = me_d // PLANE, lax.rem(me_d, PLANE)
+    me_p = me_q * tp + me_t
 
     def copy_tensor(phase, k, src, dst, slot):
         to = lax.rem(me_t + k, tp)
@@ -90,7 +94,7 @@
             device_id={"dp": lax.rem(me_d + 1, dp)}, device_id_type=MESH,
         )
 
-    STATS, DOTS, PART, WHOLE = 8, 9, 10, 11
+    STATS, DOTS = 8, 9
     rows_of = [
         (lot, lambda to, lot=lot: send_rows.at[lot, to], lambda s, lot=lot: recv_rows.at[lot, s])
         for lot in range(4)
@@ -101,12 +105,12 @@
     ]
     stats_of = (STATS, lambda to: stats, lambda s: stats_in.at[s])
     dots_of = (DOTS, lambda to: dots, lambda s: dots_in.at[s])
-    part_of = (PART, lambda to: part.at[to], lambda s: part_in.at[s])
-    whole_of = (WHOLE, lambda to: whole.at[me_t], lambda s: whole.at[s])
 
     loads = [
-        pltpu.make_async_copy(w_in_hbm, w_in, local_sem.at[0]),
-        pltpu.make_async_copy(w_out_hbm, w_out, local_sem.at[1]),
+        pltpu.make_async_copy(src, dst, local_sem.at[k])
+        for k, (src, dst) in enumerate(
+            [(tok_hbm, tok), (cot_hbm, cot), (w_in_hbm, w_in), (w_out_hbm, w_out)]
+        )
     ]
     for load in loads:
         load.start()
@@ -124,9 +128,25 @@
     greet("tensor", me_t, tp)
     greet("dp", me_d, dp)
 
+    def to_member(k):
+        member = lax.rem(me_p + k, members)
+        q, t = member // tp, lax.rem(member, tp)
+        return member, {"dp": me_z * PLANE + q, "tensor": t}
+
+    def greet_plane(k, carry):
+        q, t = lax.rem(me_q + 1 + k // (tp - 1), PLANE), lax.rem(me_t + 1 + lax.rem(k, tp - 1), tp)
+        pl.semaphore_signal(
+            barrier, inc=1, device_id={"dp": me_z * PLANE + q, "tensor": t}, device_id_type=MESH
+        )
+        return carry
+
+    others = (PLANE - 1) * (tp - 1)
+    lax.fori_loop(0, others, greet_plane, 0)
+
     row, col = iotas((c, slots))
     choose = jnp.where((row >= col * images) & (row < col * images + images), 1.0, 0.0).astype(LOW)
-    spread[...] = rows_by_rows(choose, router[...]).astype(LOW)
+    spread[...] = plain(choose, router[...]).astype(LOW)
+    loads[0].wait()
     row, col = iotas((c, n))
     begin = lax.rem(row, images) * seq
     ours = (col >= begin) & (col < begin + seq)
@@ -151,10 +171,11 @@
             send_rows[lot, t] = block.astype(LOW)
 
     cut(plain(exponent_low, tok[...]), 0)
-    pl.semaphore_wait(barrier, tp + dp - 2)
+    pl.semaphore_wait(barrier, tp + dp - 2 + others)
     start_tensor(*stats_of)
     start_tensor(*rows_of[0])
 
+    loads[1].wait()
     best = jnp.max(masked, axis=0, keepdims=True)
     raised = jnp.where(ours, jnp.exp(masked - best), 0.0)
     share = raised / jnp.sum(raised, axis=0, keepdims=True)
@@ -221,7 +242,7 @@
     row, col = iotas((c, c))
     sort = jnp.where(matching(row, col), 1.0, 0.0).astype(LOW)
     unsort = jnp.where(matching(col, row), 1.0, 0.0).astype(LOW)
-    for load in loads:
+    for load in loads[2:]:
         load.wait()
     root = math.sqrt(2.0 / math.pi)
     sorted_rows[0] = plain(sort, assembled(0)).astype(LOW)
@@ -250,13 +271,6 @@
         here = slice(e * half, (e + 1) * half)
         grad_out[e] = columns_by_columns(hidden[e], sorted_rows[1, here]).astype(LOW)
         grad_in[e] = columns_by_columns(sorted_rows[0, here], grad_pre[e]).astype(LOW)
-    stores = [
-        pltpu.make_async_copy(grad_in, grad_in_hbm, local_sem.at[2]),
-        pltpu.make_async_copy(grad_out, grad_out_hbm, local_sem.at[3]),
-    ]
-    for store in stores:
-        store.start()
-
     pass_on(summed(2), 2)
     pass_on(summed(3), 3)
     gather(2)
@@ -285,42 +299,89 @@
     fold = jnp.where((col >= row * images) & (col < row * images + images), 1.0, 0.0).astype(LOW)
     by_slot = plain(fold, grad_logits).astype(LOW)
     local_router = plain(by_slot, tok[...])
-    for t in range(tp):
-        part[t] = local_router[:, t * LANES:(t + 1) * LANES]
-    start_tensor(*part_of)
+    high = slots // PLANE
+    for q in range(PLANE):
+        for t in range(tp):
+            part[q * tp + t] = local_router[
+                q * high:(q + 1) * high, t * LANES:(t + 1) * LANES
+            ].astype(LOW)
+
+    def send_part(k, carry):
+        member, where = to_member(k)
+        pltpu.make_async_remote_copy(
+            src_ref=part.at[member], dst_ref=part_in.at[me_p],
+            send_sem=d_send.at[4], recv_sem=d_recv.at[4],
+            device_id=where, device_id_type=MESH,
+        ).start()
+        return carry
+
+    lax.fori_loop(1, members, send_part, 0)
     grad_tok[...] = (
         columns_by_columns(spots.astype(LOW), slot_grad)
         + columns_by_columns(grad_logits, spread[...])
     ).astype(LOW)
 
-    await_tensor(*part_of)
-    part_in[me_t] = part[me_t]
-    router_rows = part_in[0]
-    for s in range(1, tp):
-        router_rows = router_rows + part_in[s]
-    high = slots // dp
-    for k in range(dp):
-        piece[k] = router_rows[k * high:(k + 1) * high]
-    start_dp(4, lambda to: piece.at[to], lambda s: piece_in.at[s])
-    all_dp(4, piece, piece_in).wait_recv()
-    piece_in[me_d] = piece[me_d]
-    whole[me_t, me_d] = jnp.sum(piece_in[...], axis=0)
-    start_dp(5, lambda to: whole.at[me_t, me_d], lambda s: whole.at[me_t, s])
-    all_dp(5, whole.at[me_t], whole.at[me_t]).wait_recv()
-    start_tensor(*whole_of)
-    await_tensor(*whole_of)
-    for t in range(tp):
-        for k in range(dp):
-            grad_router[k * high:(k + 1) * high, t * LANES:(t + 1) * LANES] = whole[t, k]
-
-    for phase in [*rows_of, *slots_of, stats_of, dots_of, part_of, whole_of]:
+    def all_members(phase, out, into):
+        return pltpu.make_async_remote_copy(
+            src_ref=out.at[pl.ds(0, members - 1)], dst_ref=into.at[pl.ds(0, members - 1)],
+            send_sem=d_send.at[phase], recv_sem=d_recv.at[phase],
+            device_id=to_member(1)[1], device_id_type=MESH,
+        )
+
+    all_members(4, part, part_in).wait_recv()
+    part_in[me_p] = part[me_p]
+    piece[...] = jnp.sum(part_in[...].astype(WIDE), axis=0)
+
+    def piece_copy(k, slot):
+        return pltpu.make_async_remote_copy(
+            src_ref=piece, dst_ref=piece_in.at[slot],
+            send_sem=z_send.at[k], recv_sem=z_recv.at[k],
+            device_id={"dp": lax.rem(me_z + k, depth) * PLANE + me_q}, device_id_type=MESH,
+        )
+
+    for k in range(1, depth):
+        piece_copy(k, me_z).start()
+    for k in range(1, depth):
+        piece_copy(k, lax.rem(me_z + depth - k, depth)).wait_recv()
+    piece_in[me_z] = piece[...]
+    final[...] = jnp.sum(piece_in[...], axis=0).astype(LOW)
+
+    def send_final(k, carry):
+        pltpu.make_async_remote_copy(
+            src_ref=final, dst_ref=whole.at[me_p],
+            send_sem=d_send.at[5], recv_sem=d_recv.at[5],
+            device_id=to_member(k)[1], device_id_type=MESH,
+        ).start()
+        return carry
+
+    lax.fori_loop(1, members, send_final, 0)
+    all_members(5, whole, whole).wait_recv()
+    whole[me_p] = final[...]
+    for q in range(PLANE):
+        for t in range(tp):
+            grad_router[q * high:(q + 1) * high, t * LANES:(t + 1) * LANES] = (
+                whole[q * tp + t].astype(WIDE)
+            )
+
+    for phase in [*rows_of, *slots_of, stats_of, dots_of]:
         drain_tensor(*phase)
     for lot in range(4):
         all_dp(lot, send_slots.at[lot], recv_slots.at[lot]).wait_send()
-    all_dp(4, piece, piece_in).wait_send()
-    all_dp(5, whole.at[me_t], whole.at[me_t]).wait_send()
-    for store in stores:
-        store.wait()
+    for k in range(1, depth):
+        piece_copy(k, me_z).wait_send()
+    all_members(4, part, part_in).wait_send()
+    all_members(5, whole, whole).wait_send()
+
+
+def finish(*refs):
+    count = (len(refs) - 1) // 2
+    copies = [
+        pltpu.make_async_copy(refs[k], refs[count + k], refs[-1].at[k]) for k in range(count)
+    ]
+    for copy in copies:
+        copy.start()
+    for copy in copies:
+        copy.wait()
 
 
 def on_device(tokens, cotangent, dispatch_weight, w_in, w_out):
@@ -329,23 +390,18 @@
     own, _, inner = w_in.shape
     n, slots, group = images * seq, dp * own, own * images
     c = dp * group
-    vmem = pltpu.VMEM
+    members, high = PLANE * tp, slots // PLANE
+    vmem, hbm = pltpu.VMEM, pl.BlockSpec(memory_space=pltpu.HBM)
+    here = pl.BlockSpec(memory_space=pltpu.VMEM)
+    shapes = [((n, width), LOW), ((slots, width), WIDE), (w_in.shape, LOW), (w_out.shape, LOW)]
     outs = pl.pallas_call(
         functools.partial(kernel, tp, dp, images, own),
         name="moe_back",
-        out_shape=(
-            jax.ShapeDtypeStruct((n, width), LOW),
-            jax.ShapeDtypeStruct((slots, width), WIDE),
-            jax.ShapeDtypeStruct(w_in.shape, LOW),
-            jax.ShapeDtypeStruct(w_out.shape, LOW),
-        ),
-        in_specs=[pl.BlockSpec(memory_space=pltpu.VMEM)] * 3
-        + [pl.BlockSpec(memory_space=pl.ANY)] * 2,
-        out_specs=tuple(
-            [pl.BlockSpec(memory_space=pltpu.VMEM)] * 2 + [pl.BlockSpec(memory_space=pl.ANY)] * 2
-        ),
+        out_shape=tuple(vmem(*shape) for shape in shapes),
+        in_specs=[hbm, hbm, here, hbm, hbm],
+        out_specs=(here,) * 4,
         scratch_shapes=[
-            vmem(w_in.shape, LOW), vmem(w_out.shape, LOW),
+            vmem((n, width), LOW), vmem((n, width), LOW),
             vmem(w_in.shape, LOW), vmem(w_out.shape, LOW),
             vmem((c, width), LOW),
             vmem((c, n), WIDE), vmem((c, n), WIDE), vmem((c, n), WIDE),
@@ -356,20 +412,29 @@
             vmem((4, c, width), LOW), vmem((2, c, width), LOW),
             vmem((8, c), WIDE), vmem((tp, 8, c), WIDE),
             vmem((8, c), WIDE), vmem((tp, 8, c), WIDE),
-            vmem((tp, slots, LANES), WIDE), vmem((tp, slots, LANES), WIDE),
-            vmem((dp, slots // dp, LANES), WIDE), vmem((dp, slots // dp, LANES), WIDE),
-            vmem((tp, dp, slots // dp, LANES), WIDE),
+            vmem((members, high, LANES), LOW), vmem((members, high, LANES), LOW),
+            vmem((high, LANES), WIDE), vmem((dp // PLANE, high, LANES), WIDE),
+            vmem((members, high, LANES), LOW), vmem((high, LANES), LOW),
             pltpu.SemaphoreType.DMA((4,)),
-            pltpu.SemaphoreType.DMA((12, tp)), pltpu.SemaphoreType.DMA((12, tp)),
+            pltpu.SemaphoreType.DMA((10, tp)), pltpu.SemaphoreType.DMA((10, tp)),
             pltpu.SemaphoreType.DMA((6,)), pltpu.SemaphoreType.DMA((6,)),
+            pltpu.SemaphoreType.DMA((dp // PLANE,)), pltpu.SemaphoreType.DMA((dp // PLANE,)),
         ],
         compiler_params=pltpu.CompilerParams(
-            collective_id=0, has_side_effects=True, vmem_limit_bytes=60 * 2**20
+            collective_id=0, has_side_effects=True, vmem_limit_bytes=61400000
         ),
     )(
-        tokens.reshape(n, width), cotangent.reshape(n, width), dispatch_weight, w_in, w_out
+        tokens.reshape(n, width), cotangent.reshape(n, width), dispatch_weight.T, w_in, w_out
     )
-    grad_tokens, grad_router, grad_w_in, grad_w_out = outs
+    grad_tokens, grad_router, grad_w_in, grad_w_out = pl.pallas_call(
+        finish,
+        name="finish",
+        out_shape=tuple(jax.ShapeDtypeStruct(*shape) for shape in shapes),
+        in_specs=[here] * 4,
+        out_specs=(hbm,) * 4,
+        scratch_shapes=[pltpu.SemaphoreType.DMA((4,))],
+        compiler_params=pltpu.CompilerParams(vmem_limit_bytes=4 * 2**20),
+    )(*outs)
     return (grad_tokens.reshape(tokens.shape), grad_router.T, grad_w_in, grad_w_out)
 
 

time: 111 us -> 93.9 us (0.85)
  local copies, waits for them, and re-layouts: 9.85 us -> 0 us
  Pallas kernels: 100 us -> 93.2 us
    unnamed x7 -> x0, local copies, waits for them, and re-layouts: 9.85 us -> none
    pallas_call x1, Pallas kernels: 100 us -> 90.9 us  [on_device(): pl.pallas_call(functools.partial(kernel, tp, dp, images, own), name='moe_...]
    pallas_call x0 -> x1, Pallas kernels: none -> 2.33 us  [on_device(): pl.pallas_call(finish, name='finish', out_shape=tuple((jax.ShapeDtypeStru...]
where the time goes in v3:
time: 93.9 us; the launch traced here: 93.8 us
  Pallas kernels  93.2 us (99%)
    pallas_call x1, Pallas kernels, on_device(): pl.pallas_call(functools.partial(kernel, tp, dp, images, own), name='moe_...  90.9 us
    pallas_call x1, Pallas kernels, on_device(): pl.pallas_call(finish, name='finish', out_shape=tuple((jax.ShapeDtypeStru...  2.33 us

profile of v3, /device:TPU:1, one launch (start us, length us, event | category | flops | bytes accessed | tf_op | source)
XLA Modules:
  0.0 93.8 jit_solution(5649379071754965273)
XLA Ops:
  0.6 90.9 %moe_back.1 = (bf16[288,1024]{1,0:T(8,128)(2,1)S(1)}, f32[64,1024]{1,0:T(8,128)S(1)}, bf16[2,1024,512]{2,1,0:T(8,128)(2,1)S(1)}, bf16[2,512,1024]{2,1,0:T(8,128)(2,1)S(1)}) custom-call(bf16[288,1024]{1,0:T(8,128)(2,1)} %bitcast.5, bf16[288,1024]{1,0:T(8,128)(2,1)} %bitcast.6, bf16[64,1024]{1,0:T(8,128)(2,1)} %bitcast.7, bf16[2,1024,512]{2,1,0:T(8,128)(2,1)} %w_in_hbm.1, ...), custom_call_target="tpu_custom_call" | custom-call | tf_op jit(solution)/shard_map/moe_back/pallas_call | solution.py:397
  91.5 2.3 %finish.1 = (bf16[288,1024]{1,0:T(8,128)(2,1)}, f32[64,1024]{1,0:T(8,128)}, bf16[2,1024,512]{2,1,0:T(8,128)(2,1)}, bf16[2,512,1024]{2,1,0:T(8,128)(2,1)}) custom-call(bf16[288,1024]{1,0:T(8,128)(2,1)S(1)} %get-tuple-element.12.refs_0_, f32[64,1024]{1,0:T(8,128)S(1)} %get-tuple-element.13.refs_1_, bf16[2,1024,512]{2,1,0:T(8,128)(2,1)S(1)} %get-tuple-element.14.refs_2_, ...), custom_call_target="tpu_custom_call" | custom-call | tf_op jit(solution)/shard_map/finish/pallas_call | solution.py:429

commit v4 on v3

v4 whole, which is shorter than its diff:
```python
import functools
import math

import jax
import jax.numpy as jnp
from jax import lax
from jax.experimental import pallas as pl
from jax.experimental.pallas import tpu as pltpu
from jax.sharding import PartitionSpec as P

WIDE = jnp.float32
LOW = jnp.bfloat16
MESH = pl.DeviceIdType.MESH
LANES = 128
LEAST = -3.0e38
PLANE = 4


def dot(a, b, over):
    return lax.dot_general(a, b, (over, ((), ())), preferred_element_type=WIDE)


def plain(a, b):
    return dot(a, b, ((1,), (0,)))


def rows_by_rows(a, b):
    return dot(a, b, ((1,), (1,)))


def columns_by_columns(a, b):
    return dot(a, b, ((0,), (0,)))


def iotas(shape):
    return lax.broadcasted_iota(jnp.int32, shape, 0), lax.broadcasted_iota(jnp.int32, shape, 1)


def kernel(
    tp, dp, images, own,
    router_hbm, tok_hbm, cot_hbm, w_in_hbm, w_out_hbm,
    grad_tok, grad_router, grad_in, grad_out,
    router, tok, cot, w_in, w_out, spread, weight, combine, dispatch, slot_slice,
    send_rows, recv_rows, send_slots, recv_slots, full, flat, hidden, grad_pre, stats, stats_in,
    dots, dots_in, part, part_in, piece, piece_in, whole, final,
    local_sem, t_send, t_recv, d_send, d_recv, z_send, z_recv,
):
    me_t, me_d = lax.axis_index("tensor"), lax.axis_index("dp")
    n = tok.shape[0]
    group = own * images
    c = dp * group
    seq = n // images
    slots = dp * own
    half = c // own
    members, depth = PLANE * tp, dp // PLANE
    me_z, me_q = me_d // PLANE, lax.rem(me_d, PLANE)
    me_p = me_q * tp + me_t

    def copy_tensor(phase, k, src, dst, slot):
        to = lax.rem(me_t + k, tp)
        return pltpu.make_async_remote_copy(
            src_ref=src(to), dst_ref=dst(slot),
            send_sem=t_send.at[phase, k], recv_sem=t_recv.at[phase, k],
            device_id={"tensor": to}, device_id_type=MESH,
        )

    def start_tensor(phase, src, dst):
        for k in range(1, tp):
            copy_tensor(phase, k, src, dst, me_t).start()

    def await_tensor(phase, src, dst):
        for k in range(1, tp):
            copy_tensor(phase, k, src, dst, lax.rem(me_t + tp - k, tp)).wait_recv()

    def drain_tensor(phase, src, dst):
        for k in range(1, tp):
            copy_tensor(phase, k, src, dst, me_t).wait_send()

    def outward(k, size):
        return size // 2 + (2 * lax.rem(k, 2) - 1) * ((k + 1) // 2)

    def start_dp(phase, src, dst):
        def one(k, carry):
            to = lax.rem(me_d + outward(k, dp), dp)
            pltpu.make_async_remote_copy(
                src_ref=src(to), dst_ref=dst(me_d),
                send_sem=d_send.at[phase], recv_sem=d_recv.at[phase],
                device_id={"dp": to}, device_id_type=MESH,
            ).start()
            return carry
        lax.fori_loop(0, dp - 1, one, 0)

    def all_dp(phase, out, into):
        return pltpu.make_async_remote_copy(
            src_ref=out.at[pl.ds(0, dp - 1)], dst_ref=into.at[pl.ds(0, dp - 1)],
            send_sem=d_send.at[phase], recv_sem=d_recv.at[phase],
            device_id={"dp": lax.rem(me_d + 1, dp)}, device_id_type=MESH,
        )

    lots = [(turn, kind, e) for turn in range(2) for kind in range(2) for e in range(own)]
    number = {lot: k for k, lot in enumerate(lots)}
    STATS, DOTS = 2 * len(lots), 2 * len(lots) + 1
    rows_of = [
        (k, lambda to, k=k: send_rows.at[k, to], lambda s, k=k: recv_rows.at[k, s])
        for k in range(len(lots))
    ]
    slots_of = [
        (len(lots) + k, lambda to, k=k: recv_slots.at[k], lambda s, k=k: full.at[k, s])
        for k in range(len(lots))
    ]
    stats_of = (STATS, lambda to: stats, lambda s: stats_in.at[s])
    dots_of = (DOTS, lambda to: dots, lambda s: dots_in.at[s])

    loads = [
        pltpu.make_async_copy(src, dst, local_sem.at[k])
        for k, (src, dst) in enumerate(
            [
                (router_hbm, router), (tok_hbm, tok), (cot_hbm, cot),
                (w_in_hbm, w_in), (w_out_hbm, w_out),
            ]
        )
    ]
    for load in loads:
        load.start()

    barrier = pltpu.get_barrier_semaphore()

    def greet_dp(k, carry):
        pl.semaphore_signal(
            barrier, inc=1, device_id={"dp": lax.rem(me_d + outward(k, dp), dp)},
            device_id_type=MESH,
        )
        return carry

    lax.fori_loop(0, dp - 1, greet_dp, 0)

    def to_member(k):
        member = lax.rem(me_p + k, members)
        q, t = member // tp, lax.rem(member, tp)
        return member, {"dp": me_z * PLANE + q, "tensor": t}

    def greet_plane(k, carry):
        q, t = lax.rem(me_q + 1 + k // (tp - 1), PLANE), lax.rem(me_t + 1 + lax.rem(k, tp - 1), tp)
        pl.semaphore_signal(
            barrier, inc=1, device_id={"dp": me_z * PLANE + q, "tensor": t}, device_id_type=MESH
        )
        return carry

    others = (PLANE - 1) * (tp - 1)
    lax.fori_loop(0, others, greet_plane, 0)
    for k in range(1, tp):
        pl.semaphore_signal(
            barrier, inc=1, device_id={"tensor": lax.rem(me_t + k, tp)}, device_id_type=MESH
        )

    def belongs(slot, at):
        e = lax.rem(slot, own)
        first = e * half + (slot - e) * (images // own)
        return (at >= first) & (at < first + images)

    row, col = iotas((c, slots))
    choose = jnp.where(belongs(col, row), 1.0, 0.0).astype(LOW)
    loads[0].wait()
    spread[...] = plain(choose, router[...]).astype(LOW)
    loads[1].wait()
    row, col = iotas((c, n))
    begin = lax.rem(row, images) * seq
    ours = (col >= begin) & (col < begin + seq)
    masked = jnp.where(ours, rows_by_rows(spread[...], tok[...]), LEAST)
    top = jnp.max(masked, axis=1, keepdims=True)
    exponent = jnp.where(ours, jnp.exp(masked - top), 0.0)
    exponent_low = exponent.astype(LOW)
    weight[...] = exponent
    lane = iotas((c, LANES))[1]
    packed = jnp.where(
        lane == 0, top,
        jnp.where(
            lane == 1, jnp.sum(exponent, axis=1, keepdims=True),
            jnp.sum(exponent_low.astype(WIDE), axis=1, keepdims=True),
        ),
    )
    stats[...] = jnp.transpose(packed)[0:8, :]

    def cut(rows, lot):
        for t in range(tp):
            block = rows[:, t * LANES:(t + 1) * LANES].reshape(dp, images, LANES)
            send_rows[number[lot], t] = block.astype(LOW)

    def begin_sum(rows, lot):
        cut(rows, lot)
        start_tensor(*rows_of[number[lot]])

    cut(plain(exponent_low[0:half], tok[...]), (0, 0, 0))
    pl.semaphore_wait(barrier, tp + dp - 2 + others)
    start_tensor(*stats_of)
    start_tensor(*rows_of[0])
    for e in range(1, own):
        begin_sum(plain(exponent_low[e * half:(e + 1) * half], tok[...]), (0, 0, e))

    loads[2].wait()
    best = jnp.max(masked, axis=0, keepdims=True)
    raised = jnp.where(ours, jnp.exp(masked - best), 0.0)
    share = raised / jnp.sum(raised, axis=0, keepdims=True)
    combine[...] = share
    share_low = share.astype(LOW)
    for e in range(own):
        begin_sum(plain(share_low[e * half:(e + 1) * half], cot[...]), (0, 1, e))

    await_tensor(*stats_of)
    stats_in[me_t] = stats[...]
    most = stats_in[0, 0:1]
    for s in range(1, tp):
        most = jnp.maximum(most, stats_in[s, 0:1])
    shrinks = [jnp.exp(stats_in[s, 0:1] - most) for s in range(tp)]
    total = sum(stats_in[s, 1:2] * shrinks[s] for s in range(tp))
    total_low = sum(stats_in[s, 2:3] * shrinks[s] for s in range(tp))
    lines = [shrink / total_low for shrink in shrinks]
    lines.append(jnp.exp(stats[0:1] - most) / total)
    line_row = iotas((LANES, c))[0]
    table = jnp.zeros((LANES, c), WIDE)
    for s, line in enumerate(lines):
        table = jnp.where(line_row == s, line, table)
    table = jnp.transpose(table)
    dispatch[...] = weight[...] * table[:, tp:tp + 1]

    def pass_on(lot):
        k, e = number[lot], lot[2]
        await_tensor(*rows_of[k])
        recv_rows[k, me_t] = send_rows[k, me_t]
        total_rows = None
        for s in range(tp):
            term = recv_rows[k, s].astype(WIDE).reshape(half, LANES)
            if lot[:2] == (0, 0):
                term = term * table[e * half:(e + 1) * half, s:s + 1]
            total_rows = term if total_rows is None else total_rows + term
        if lot[:2] == (0, 0):
            slot_slice[e * half:(e + 1) * half] = total_rows
        send_slots[k] = total_rows.reshape(dp, images, LANES).astype(LOW)
        start_dp(k, lambda to: send_slots.at[k, to], lambda s: recv_slots.at[k, s])

    def gather(lot):
        k = number[lot]
        all_dp(k, send_slots.at[k], recv_slots.at[k]).wait_recv()
        recv_slots[k, me_d] = send_slots[k, me_d]
        start_tensor(*slots_of[k])

    def assembled(lot):
        k, (turn, kind, e) = number[lot], lot
        await_tensor(*slots_of[k])
        full[k, me_t] = recv_slots[k]
        for t in range(tp):
            block = full[k, t].astype(WIDE).reshape(half, LANES)
            flat[turn, kind, e * half:(e + 1) * half, t * LANES:(t + 1) * LANES] = (
                block.astype(LOW)
            )
        return flat[turn, kind, e * half:(e + 1) * half]

    root = math.sqrt(2.0 / math.pi)
    slope = {}

    def expert_out(e):
        pre = plain(assembled((0, 0, e)), w_in[e])
        square = pre * pre
        bent = jnp.tanh(root * (pre + 0.044715 * (square * pre)))
        hidden[e] = (0.5 * pre * (1.0 + bent)).astype(LOW)
        slope[e] = 0.5 * (1.0 + bent) + 0.5 * pre * (1.0 - bent * bent) * (
            root * (1.0 + 3.0 * 0.044715 * square)
        )
        begin_sum(plain(hidden[e], w_out[e]), (1, 0, e))

    def expert_back(e):
        grad_hidden = rows_by_rows(assembled((0, 1, e)), w_out[e])
        grad_pre[e] = (slope[e] * grad_hidden).astype(LOW)
        begin_sum(rows_by_rows(grad_pre[e], w_in[e]), (1, 1, e))

    pass_on((0, 0, 0))
    pass_on((0, 0, 1))
    pass_on((0, 1, 0))
    gather((0, 0, 0))
    pass_on((0, 1, 1))
    gather((0, 0, 1))
    gather((0, 1, 0))
    for load in loads[3:]:
        load.wait()
    gather((0, 1, 1))
    expert_out(0)
    expert_out(1)
    expert_back(0)
    expert_back(1)
    pass_on((1, 0, 0))
    pass_on((1, 0, 1))
    pass_on((1, 1, 0))
    gather((1, 0, 0))
    pass_on((1, 1, 1))
    gather((1, 0, 1))
    gather((1, 1, 0))
    gather((1, 1, 1))
    products = jnp.concatenate([
        recv_slots[number[(1, 1, e)]].astype(WIDE).reshape(half, LANES) for e in range(own)
    ]) * slot_slice[...]
    own_dots = jnp.broadcast_to(jnp.sum(products, axis=1, keepdims=True), (c, LANES))
    dots[...] = jnp.transpose(own_dots)[0:8, :]
    start_tensor(*dots_of)
    for e in range(own):
        here = slice(e * half, (e + 1) * half)
        grad_out[e] = columns_by_columns(hidden[e], flat[0, 1, here]).astype(LOW)
        grad_in[e] = columns_by_columns(flat[0, 0, here], grad_pre[e]).astype(LOW)

    share = combine[...]
    grad_share = jnp.concatenate(
        [rows_by_rows(assembled((1, 0, e)), cot[...]) for e in range(own)]
    )
    row_dot = jnp.sum(grad_share * share, axis=0, keepdims=True)
    from_share = share * (grad_share - row_dot)
    grad_weight = jnp.concatenate(
        [rows_by_rows(assembled((1, 1, e)), tok[...]) for e in range(own)]
    )
    slot_grad = flat[1, 1]
    await_tensor(*dots_of)
    dots_in[me_t] = dots[...]
    dot_line = dots_in[0, 0:1]
    for s in range(1, tp):
        dot_line = dot_line + dots_in[s, 0:1]
    column_dot = jnp.transpose(jnp.broadcast_to(dot_line, (LANES, c)))[:, 0:1]
    spots = dispatch[...]
    grad_logits = (from_share + spots * (grad_weight - column_dot)).astype(LOW)
    row, col = iotas((slots, c))
    fold = jnp.where(belongs(row, col), 1.0, 0.0).astype(LOW)
    by_slot = plain(fold, grad_logits).astype(LOW)
    local_router = plain(by_slot, tok[...])
    high = slots // PLANE
    for q in range(PLANE):
        for t in range(tp):
            part[q * tp + t] = local_router[
                q * high:(q + 1) * high, t * LANES:(t + 1) * LANES
            ].astype(LOW)

    def send_part(k, carry):
        member, where = to_member(k)
        pltpu.make_async_remote_copy(
            src_ref=part.at[member], dst_ref=part_in.at[me_p],
            send_sem=d_send.at[8], recv_sem=d_recv.at[8],
            device_id=where, device_id_type=MESH,
        ).start()
        return carry

    lax.fori_loop(1, members, send_part, 0)
    grad_tok[...] = (
        columns_by_columns(spots.astype(LOW), slot_grad)
        + columns_by_columns(grad_logits, spread[...])
    ).astype(LOW)

    def all_members(phase, out, into):
        return pltpu.make_async_remote_copy(
            src_ref=out.at[pl.ds(0, members - 1)], dst_ref=into.at[pl.ds(0, members - 1)],
            send_sem=d_send.at[phase], recv_sem=d_recv.at[phase],
            device_id=to_member(1)[1], device_id_type=MESH,
        )

    all_members(8, part, part_in).wait_recv()
    part_in[me_p] = part[me_p]
    piece[...] = jnp.sum(part_in[...].astype(WIDE), axis=0)

    def piece_copy(k, slot):
        return pltpu.make_async_remote_copy(
            src_ref=piece, dst_ref=piece_in.at[slot],
            send_sem=z_send.at[k], recv_sem=z_recv.at[k],
            device_id={"dp": lax.rem(me_z + k, depth) * PLANE + me_q}, device_id_type=MESH,
        )

    for k in range(1, depth):
        piece_copy(k, me_z).start()
    for k in range(1, depth):
        piece_copy(k, lax.rem(me_z + depth - k, depth)).wait_recv()
    piece_in[me_z] = piece[...]
    final[...] = jnp.sum(piece_in[...], axis=0).astype(LOW)

    def send_final(k, carry):
        pltpu.make_async_remote_copy(
            src_ref=final, dst_ref=whole.at[me_p],
            send_sem=d_send.at[9], recv_sem=d_recv.at[9],
            device_id=to_member(k)[1], device_id_type=MESH,
        ).start()
        return carry

    lax.fori_loop(1, members, send_final, 0)
    all_members(9, whole, whole).wait_recv()
    whole[me_p] = final[...]
    for q in range(PLANE):
        for t in range(tp):
            grad_router[q * high:(q + 1) * high, t * LANES:(t + 1) * LANES] = (
                whole[q * tp + t].astype(WIDE)
            )

    for phase in [*rows_of, *slots_of, stats_of, dots_of]:
        drain_tensor(*phase)
    for k in range(len(lots)):
        all_dp(k, send_slots.at[k], recv_slots.at[k]).wait_send()
    for k in range(1, depth):
        piece_copy(k, me_z).wait_send()
    all_members(8, part, part_in).wait_send()
    all_members(9, whole, whole).wait_send()


def finish(*refs):
    count = (len(refs) - 1) // 2
    copies = [
        pltpu.make_async_copy(refs[k], refs[count + k], refs[-1].at[k]) for k in range(count)
    ]
    for copy in copies:
        copy.start()
    for copy in copies:
        copy.wait()


def on_device(tokens, cotangent, dispatch_weight, w_in, w_out):
    tp, dp = lax.axis_size("tensor"), lax.axis_size("dp")
    images, seq, width = tokens.shape
    own, _, inner = w_in.shape
    n, slots, group = images * seq, dp * own, own * images
    c = dp * group
    members, high, lots = PLANE * tp, slots // PLANE, 4 * own
    vmem, hbm = pltpu.VMEM, pl.BlockSpec(memory_space=pltpu.HBM)
    here = pl.BlockSpec(memory_space=pltpu.VMEM)
    shapes = [((n, width), LOW), ((slots, width), WIDE), (w_in.shape, LOW), (w_out.shape, LOW)]
    outs = pl.pallas_call(
        functools.partial(kernel, tp, dp, images, own),
        name="moe_back",
        out_shape=tuple(vmem(*shape) for shape in shapes),
        in_specs=[hbm] * 5,
        out_specs=(here,) * 4,
        scratch_shapes=[
            vmem((slots, width), LOW), vmem((n, width), LOW), vmem((n, width), LOW),
            vmem(w_in.shape, LOW), vmem(w_out.shape, LOW),
            vmem((c, width), LOW),
            vmem((c, n), WIDE), vmem((c, n), WIDE), vmem((c, n), WIDE),
            vmem((c, LANES), WIDE),
            vmem((lots, tp, dp, images, LANES), LOW), vmem((lots, tp, dp, images, LANES), LOW),
            vmem((lots, dp, images, LANES), LOW), vmem((lots, dp, images, LANES), LOW),
            vmem((lots, tp, dp, images, LANES), LOW),
            vmem((2, 2, c, width), LOW),
            vmem((own, c // own, inner), LOW), vmem((own, c // own, inner), LOW),
            vmem((8, c), WIDE), vmem((tp, 8, c), WIDE),
            vmem((8, c), WIDE), vmem((tp, 8, c), WIDE),
            vmem((members, high, LANES), LOW), vmem((members, high, LANES), LOW),
            vmem((high, LANES), WIDE), vmem((dp // PLANE, high, LANES), WIDE),
            vmem((members, high, LANES), LOW), vmem((high, LANES), LOW),
            pltpu.SemaphoreType.DMA((5,)),
            pltpu.SemaphoreType.DMA((2 * lots + 2, tp)), pltpu.SemaphoreType.DMA((2 * lots + 2, tp)),
            pltpu.SemaphoreType.DMA((lots + 2,)), pltpu.SemaphoreType.DMA((lots + 2,)),
            pltpu.SemaphoreType.DMA((dp // PLANE,)), pltpu.SemaphoreType.DMA((dp // PLANE,)),
        ],
        compiler_params=pltpu.CompilerParams(
            collective_id=0, has_side_effects=True, vmem_limit_bytes=61400000
        ),
    )(
        dispatch_weight.T, tokens.reshape(n, width), cotangent.reshape(n, width), w_in, w_out
    )
    grad_tokens, grad_router, grad_w_in, grad_w_out = pl.pallas_call(
        finish,
        name="finish",
        out_shape=tuple(jax.ShapeDtypeStruct(*shape) for shape in shapes),
        in_specs=[here] * 4,
        out_specs=(hbm,) * 4,
        scratch_shapes=[pltpu.SemaphoreType.DMA((4,))],
        compiler_params=pltpu.CompilerParams(vmem_limit_bytes=4 * 2**20),
    )(*outs)
    return (grad_tokens.reshape(tokens.shape), grad_router.T, grad_w_in, grad_w_out)


def solution(mesh):
    return jax.shard_map(
        on_device,
        mesh=mesh,
        in_specs=(
            P("dp", "tensor", None),
            P("dp", "tensor", None),
            P(),
            P("dp", None, "tensor"),
            P("dp", "tensor", None),
        ),
        out_specs=(P("dp", "tensor", None), P(), P("dp", None, "tensor"), P("dp", "tensor", None)),
        check_vma=False,
    )
```

time: 93.9 us -> 90.1 us (0.960)
  Pallas kernels: 93.2 us -> 89.4 us
    pallas_call x1, Pallas kernels: 90.9 us -> 87.1 us  [on_device(): pl.pallas_call(functools.partial(kernel, tp, dp, images, own), name='moe_...]
where the time goes in v4:
time: 90.1 us; the launch traced here: 90 us
  Pallas kernels  89.4 us (99%)
    pallas_call x1, Pallas kernels, on_device(): pl.pallas_call(functools.partial(kernel, tp, dp, images, own), name='moe_...  87.1 us
    pallas_call x1, Pallas kernels, on_device(): pl.pallas_call(finish, name='finish', out_shape=tuple((jax.ShapeDtypeStru...  2.33 us

profile of v4, /device:TPU:1, one launch (start us, length us, event | category | flops | bytes accessed | tf_op | source)
XLA Modules:
  0.0 90.0 jit_solution(12447862279900214355)
XLA Ops:
  0.6 87.1 %moe_back.1 = (bf16[288,1024]{1,0:T(8,128)(2,1)S(1)}, f32[64,1024]{1,0:T(8,128)S(1)}, bf16[2,1024,512]{2,1,0:T(8,128)(2,1)S(1)}, bf16[2,512,1024]{2,1,0:T(8,128)(2,1)S(1)}) custom-call(bf16[64,1024]{1,0:T(8,128)(2,1)} %bitcast.7, bf16[288,1024]{1,0:T(8,128)(2,1)} %bitcast.5, bf16[288,1024]{1,0:T(8,128)(2,1)} %bitcast.6, bf16[2,1024,512]{2,1,0:T(8,128)(2,1)} %w_in_hbm.1, ...), custom_call_target="tpu_custom_call" | custom-call | tf_op jit(solution)/shard_map/moe_back/pallas_call | solution.py:426
  87.7 2.3 %finish.1 = (bf16[288,1024]{1,0:T(8,128)(2,1)}, f32[64,1024]{1,0:T(8,128)}, bf16[2,1024,512]{2,1,0:T(8,128)(2,1)}, bf16[2,512,1024]{2,1,0:T(8,128)(2,1)}) custom-call(bf16[288,1024]{1,0:T(8,128)(2,1)S(1)} %get-tuple-element.12.refs_0_, f32[64,1024]{1,0:T(8,128)S(1)} %get-tuple-element.13.refs_1_, bf16[2,1024,512]{2,1,0:T(8,128)(2,1)S(1)} %get-tuple-element.14.refs_2_, ...), custom_call_target="tpu_custom_call" | custom-call | tf_op jit(solution)/shard_map/finish/pallas_call | solution.py:459

commit v5 on v4

--- a/solution.py
+++ b/solution.py
@@ -41,9 +41,11 @@
     router_hbm, tok_hbm, cot_hbm, w_in_hbm, w_out_hbm,
     grad_tok, grad_router, grad_in, grad_out,
     router, tok, cot, w_in, w_out, spread, weight, combine, dispatch, slot_slice,
-    send_rows, recv_rows, send_slots, recv_slots, full, flat, hidden, grad_pre, stats, stats_in,
+    out_send, out_recv, back_send, back_recv, send_slots, slots_out, slots_back,
+    full_out, full_back, flat, hidden, grad_pre,
+    stats, stats_in,
     dots, dots_in, part, part_in, piece, piece_in, whole, final,
-    local_sem, t_send, t_recv, d_send, d_recv, z_send, z_recv,
+    local_sem, t_send, t_recv, p_send, p_recv, z_send, z_recv,
 ):
     me_t, me_d = lax.axis_index("tensor"), lax.axis_index("dp")
     n = tok.shape[0]
@@ -65,49 +67,95 @@
         )
 
     def start_tensor(phase, src, dst):
-        for k in range(1, tp):
+        for k in sorted(range(1, tp), key=lambda k: -min(k, tp - k)):
             copy_tensor(phase, k, src, dst, me_t).start()
+
+    def before(k):
+        return lax.rem(me_t + tp - k, tp)
+
+    def await_one(k, phase, src, dst):
+        copy_tensor(phase, k, src, dst, before(k)).wait_recv()
 
     def await_tensor(phase, src, dst):
         for k in range(1, tp):
-            copy_tensor(phase, k, src, dst, lax.rem(me_t + tp - k, tp)).wait_recv()
+            await_one(k, phase, src, dst)
 
     def drain_tensor(phase, src, dst):
         for k in range(1, tp):
             copy_tensor(phase, k, src, dst, me_t).wait_send()
 
-    def outward(k, size):
-        return size // 2 + (2 * lax.rem(k, 2) - 1) * ((k + 1) // 2)
-
-    def start_dp(phase, src, dst):
-        def one(k, carry):
-            to = lax.rem(me_d + outward(k, dp), dp)
-            pltpu.make_async_remote_copy(
-                src_ref=src(to), dst_ref=dst(me_d),
-                send_sem=d_send.at[phase], recv_sem=d_recv.at[phase],
-                device_id={"dp": to}, device_id_type=MESH,
+    def remote(src, dst, send_sem, recv_sem, where):
+        return pltpu.make_async_remote_copy(
+            src_ref=src, dst_ref=dst, send_sem=send_sem, recv_sem=recv_sem,
+            device_id=where, device_id_type=MESH,
+        )
+
+    near = [
+        (lax.rem(me_q + jq, PLANE), lax.rem(me_t + jt, tp))
+        for jt in sorted(range(tp), key=lambda jt: -min(jt, tp - jt))
+        for jq in sorted(range(PLANE), key=lambda jq: -min(jq, PLANE - jq))
+        if (jq, jt) != (0, 0)
+    ]
+
+    def start_plane(phase, src, dst):
+        for q, t in near:
+            remote(
+                src(q, t), dst, p_send.at[phase], p_recv.at[phase],
+                {"dp": me_z * PLANE + q, "tensor": t},
             ).start()
-            return carry
-        lax.fori_loop(0, dp - 1, one, 0)
-
-    def all_dp(phase, out, into):
-        return pltpu.make_async_remote_copy(
-            src_ref=out.at[pl.ds(0, dp - 1)], dst_ref=into.at[pl.ds(0, dp - 1)],
-            send_sem=d_send.at[phase], recv_sem=d_recv.at[phase],
-            device_id={"dp": lax.rem(me_d + 1, dp)}, device_id_type=MESH,
-        )
+
+    def all_plane(phase, blocks):
+        few = pl.ds(0, members - 1)
+        q, t = near[0]
+        return remote(
+            blocks.at[few], blocks.at[few], p_send.at[phase], p_recv.at[phase],
+            {"dp": me_z * PLANE + q, "tensor": t},
+        )
+
+    def z_copy(phase, k, src, dst, slot):
+        to = lax.rem(me_z + k, depth)
+        return remote(
+            src(to), dst(slot), z_send.at[phase, k], z_recv.at[phase, k],
+            {"dp": to * PLANE + me_q},
+        )
+
+    def start_z(phase, src, dst):
+        for k in sorted(range(1, depth), key=lambda k: -min(k, depth - k)):
+            z_copy(phase, k, src, dst, me_z).start()
+
+    def await_z(phase, src, dst):
+        for k in range(1, depth):
+            z_copy(phase, k, src, dst, lax.rem(me_z + depth - k, depth)).wait_recv()
+
+    def drain_z(phase, src, dst):
+        for k in range(1, depth):
+            z_copy(phase, k, src, dst, me_z).wait_send()
 
     lots = [(turn, kind, e) for turn in range(2) for kind in range(2) for e in range(own)]
     number = {lot: k for k, lot in enumerate(lots)}
-    STATS, DOTS = 2 * len(lots), 2 * len(lots) + 1
-    rows_of = [
-        (k, lambda to, k=k: send_rows.at[k, to], lambda s, k=k: recv_rows.at[k, s])
-        for k in range(len(lots))
-    ]
-    slots_of = [
-        (len(lots) + k, lambda to, k=k: recv_slots.at[k], lambda s, k=k: full.at[k, s])
-        for k in range(len(lots))
-    ]
+    STATS, DOTS = len(lots), len(lots) + 1
+    ways = len(lots) // 2
+    tensor_of = [
+        (k, lambda to, k=k: out_send.at[k, to], lambda s, k=k: out_recv.at[k, s])
+        for k in range(ways)
+    ] + [
+        (ways + k, lambda to, k=k: slots_back.at[k], lambda s, k=k: full_back.at[k, s])
+        for k in range(ways)
+    ]
+    plane_of = [
+        (k, lambda q, t, k=k: slots_out.at[k, q], full_out.at[k, me_p]) for k in range(ways)
+    ] + [
+        (ways + k, lambda q, t, k=k: back_send.at[k, q * tp + t], back_recv.at[k, me_p])
+        for k in range(ways)
+    ]
+    z_of = [
+        (k, lambda to, k=k: send_slots.at[k, to], lambda s, k=k: slots_out.at[k, :, s])
+        for k in range(ways)
+    ] + [
+        (k, lambda to, k=k: send_slots.at[k, to], lambda s, k=k: slots_back.at[k - ways, s])
+        for k in range(ways, 2 * ways)
+    ]
+    PART, WHOLE, PIECE = 2 * ways, 2 * ways + 1, 2 * ways
     stats_of = (STATS, lambda to: stats, lambda s: stats_in.at[s])
     dots_of = (DOTS, lambda to: dots, lambda s: dots_in.at[s])
 
@@ -125,32 +173,14 @@
 
     barrier = pltpu.get_barrier_semaphore()
 
-    def greet_dp(k, carry):
+    for k in sorted(range(1, depth), key=lambda k: -min(k, depth - k)):
         pl.semaphore_signal(
-            barrier, inc=1, device_id={"dp": lax.rem(me_d + outward(k, dp), dp)},
+            barrier, inc=1, device_id={"dp": lax.rem(me_z + k, depth) * PLANE + me_q},
             device_id_type=MESH,
         )
-        return carry
-
-    lax.fori_loop(0, dp - 1, greet_dp, 0)
-
-    def to_member(k):
-        member = lax.rem(me_p + k, members)
-        q, t = member // tp, lax.rem(member, tp)
-        return member, {"dp": me_z * PLANE + q, "tensor": t}
-
-    def greet_plane(k, carry):
-        q, t = lax.rem(me_q + 1 + k // (tp - 1), PLANE), lax.rem(me_t + 1 + lax.rem(k, tp - 1), tp)
+    for q, t in near:
         pl.semaphore_signal(
             barrier, inc=1, device_id={"dp": me_z * PLANE + q, "tensor": t}, device_id_type=MESH
-        )
-        return carry
-
-    others = (PLANE - 1) * (tp - 1)
-    lax.fori_loop(0, others, greet_plane, 0)
-    for k in range(1, tp):
-        pl.semaphore_signal(
-            barrier, inc=1, device_id={"tensor": lax.rem(me_t + k, tp)}, device_id_type=MESH
         )
 
     def belongs(slot, at):
@@ -181,19 +211,30 @@
     )
     stats[...] = jnp.transpose(packed)[0:8, :]
 
+    across = depth * images
+
     def cut(rows, lot):
+        k = number[lot]
         for t in range(tp):
-            block = rows[:, t * LANES:(t + 1) * LANES].reshape(dp, images, LANES)
-            send_rows[number[lot], t] = block.astype(LOW)
+            block = rows[:, t * LANES:(t + 1) * LANES]
+            if lot[0] == 0:
+                out_send[k, t] = block.reshape(dp, images, LANES).astype(LOW)
+            else:
+                for q in range(PLANE):
+                    share = block[q * across:(q + 1) * across].reshape(depth, images, LANES)
+                    back_send[k - ways, q * tp + t] = share.astype(LOW)
 
     def begin_sum(rows, lot):
         cut(rows, lot)
-        start_tensor(*rows_of[number[lot]])
+        if lot[0] == 0:
+            start_tensor(*tensor_of[number[lot]])
+        else:
+            start_plane(*plane_of[number[lot]])
 
     cut(plain(exponent_low[0:half], tok[...]), (0, 0, 0))
-    pl.semaphore_wait(barrier, tp + dp - 2 + others)
+    pl.semaphore_wait(barrier, members + depth - 2)
     start_tensor(*stats_of)
-    start_tensor(*rows_of[0])
+    start_tensor(*tensor_of[0])
     for e in range(1, own):
         begin_sum(plain(exponent_low[e * half:(e + 1) * half], tok[...]), (0, 0, e))
 
@@ -214,7 +255,10 @@
     shrinks = [jnp.exp(stats_in[s, 0:1] - most) for s in range(tp)]
     total = sum(stats_in[s, 1:2] * shrinks[s] for s in range(tp))
     total_low = sum(stats_in[s, 2:3] * shrinks[s] for s in range(tp))
-    lines = [shrink / total_low for shrink in shrinks]
+    lines = [
+        jnp.exp((stats_in[before(k), 0:1] if k else stats[0:1]) - most) / total_low
+        for k in range(tp)
+    ]
     lines.append(jnp.exp(stats[0:1] - most) / total)
     line_row = iotas((LANES, c))[0]
     table = jnp.zeros((LANES, c), WIDE)
@@ -225,34 +269,59 @@
 
     def pass_on(lot):
         k, e = number[lot], lot[2]
-        await_tensor(*rows_of[k])
-        recv_rows[k, me_t] = send_rows[k, me_t]
-        total_rows = None
-        for s in range(tp):
-            term = recv_rows[k, s].astype(WIDE).reshape(half, LANES)
-            if lot[:2] == (0, 0):
-                term = term * table[e * half:(e + 1) * half, s:s + 1]
-            total_rows = term if total_rows is None else total_rows + term
-        if lot[:2] == (0, 0):
-            slot_slice[e * half:(e + 1) * half] = total_rows
-        send_slots[k] = total_rows.reshape(dp, images, LANES).astype(LOW)
-        start_dp(k, lambda to: send_slots.at[k, to], lambda s: recv_slots.at[k, s])
+        if lot[0] == 0:
+            total_rows = None
+            for back in range(tp):
+                if back:
+                    await_one(back, *tensor_of[k])
+                    term = out_recv[k, before(back)]
+                else:
+                    term = out_send[k, me_t]
+                term = term.astype(WIDE).reshape(half, LANES)
+                if lot[1] == 0:
+                    term = term * table[e * half:(e + 1) * half, back:back + 1]
+                total_rows = term if total_rows is None else total_rows + term
+            if lot[1] == 0:
+                slot_slice[e * half:(e + 1) * half] = total_rows
+            send_slots[k] = total_rows.reshape(depth, PLANE, images, LANES).astype(LOW)
+        else:
+            all_plane(k, back_recv.at[k - ways]).wait_recv()
+            back_recv[k - ways, me_p] = back_send[k - ways, me_p]
+            for q in range(PLANE):
+                total_rows = back_recv[k - ways, q * tp].astype(WIDE)
+                for t in range(1, tp):
+                    total_rows = total_rows + back_recv[k - ways, q * tp + t].astype(WIDE)
+                send_slots[k, :, q] = total_rows.astype(LOW)
+        start_z(*z_of[k])
 
     def gather(lot):
         k = number[lot]
-        all_dp(k, send_slots.at[k], recv_slots.at[k]).wait_recv()
-        recv_slots[k, me_d] = send_slots[k, me_d]
-        start_tensor(*slots_of[k])
+        await_z(*z_of[k])
+        if lot[0] == 0:
+            slots_out[k, :, me_z] = send_slots[k, me_z]
+            start_plane(*plane_of[k])
+        else:
+            slots_back[k - ways, me_z] = send_slots[k, me_z]
+            start_tensor(*tensor_of[k])
 
     def assembled(lot):
         k, (turn, kind, e) = number[lot], lot
-        await_tensor(*slots_of[k])
-        full[k, me_t] = recv_slots[k]
-        for t in range(tp):
-            block = full[k, t].astype(WIDE).reshape(half, LANES)
-            flat[turn, kind, e * half:(e + 1) * half, t * LANES:(t + 1) * LANES] = (
-                block.astype(LOW)
-            )
+        if turn == 0:
+            all_plane(k, full_out.at[k]).wait_recv()
+            full_out[k, me_p] = slots_out[k, me_q]
+            for q in range(PLANE):
+                rows = slice(e * half + q * across, e * half + (q + 1) * across)
+                for t in range(tp):
+                    block = full_out[k, q * tp + t].astype(WIDE).reshape(across, LANES)
+                    flat[turn, kind, rows, t * LANES:(t + 1) * LANES] = block.astype(LOW)
+        else:
+            await_tensor(*tensor_of[k])
+            full_back[k - ways, me_t] = slots_back[k - ways]
+            for t in range(tp):
+                block = full_back[k - ways, t].astype(WIDE).reshape(half, LANES)
+                flat[turn, kind, e * half:(e + 1) * half, t * LANES:(t + 1) * LANES] = (
+                    block.astype(LOW)
+                )
         return flat[turn, kind, e * half:(e + 1) * half]
 
     root = math.sqrt(2.0 / math.pi)
@@ -296,7 +365,7 @@
     gather((1, 1, 0))
     gather((1, 1, 1))
     products = jnp.concatenate([
-        recv_slots[number[(1, 1, e)]].astype(WIDE).reshape(half, LANES) for e in range(own)
+        slots_back[number[(1, 1, e)] - ways].astype(WIDE).reshape(half, LANES) for e in range(own)
     ]) * slot_slice[...]
     own_dots = jnp.broadcast_to(jnp.sum(products, axis=1, keepdims=True), (c, LANES))
     dots[...] = jnp.transpose(own_dots)[0:8, :]
@@ -335,56 +404,22 @@
                 q * high:(q + 1) * high, t * LANES:(t + 1) * LANES
             ].astype(LOW)
 
-    def send_part(k, carry):
-        member, where = to_member(k)
-        pltpu.make_async_remote_copy(
-            src_ref=part.at[member], dst_ref=part_in.at[me_p],
-            send_sem=d_send.at[8], recv_sem=d_recv.at[8],
-            device_id=where, device_id_type=MESH,
-        ).start()
-        return carry
-
-    lax.fori_loop(1, members, send_part, 0)
+    start_plane(PART, lambda q, t: part.at[q * tp + t], part_in.at[me_p])
     grad_tok[...] = (
         columns_by_columns(spots.astype(LOW), slot_grad)
         + columns_by_columns(grad_logits, spread[...])
     ).astype(LOW)
 
-    def all_members(phase, out, into):
-        return pltpu.make_async_remote_copy(
-            src_ref=out.at[pl.ds(0, members - 1)], dst_ref=into.at[pl.ds(0, members - 1)],
-            send_sem=d_send.at[phase], recv_sem=d_recv.at[phase],
-            device_id=to_member(1)[1], device_id_type=MESH,
-        )
-
-    all_members(8, part, part_in).wait_recv()
+    all_plane(PART, part_in).wait_recv()
     part_in[me_p] = part[me_p]
     piece[...] = jnp.sum(part_in[...].astype(WIDE), axis=0)
-
-    def piece_copy(k, slot):
-        return pltpu.make_async_remote_copy(
-            src_ref=piece, dst_ref=piece_in.at[slot],
-            send_sem=z_send.at[k], recv_sem=z_recv.at[k],
-            device_id={"dp": lax.rem(me_z + k, depth) * PLANE + me_q}, device_id_type=MESH,
-        )
-
-    for k in range(1, depth):
-        piece_copy(k, me_z).start()
-    for k in range(1, depth):
-        piece_copy(k, lax.rem(me_z + depth - k, depth)).wait_recv()
+    piece_of = (PIECE, lambda to: piece, lambda s: piece_in.at[s])
+    start_z(*piece_of)
+    await_z(*piece_of)
     piece_in[me_z] = piece[...]
     final[...] = jnp.sum(piece_in[...], axis=0).astype(LOW)
-
-    def send_final(k, carry):
-        pltpu.make_async_remote_copy(
-            src_ref=final, dst_ref=whole.at[me_p],
-            send_sem=d_send.at[9], recv_sem=d_recv.at[9],
-            device_id=to_member(k)[1], device_id_type=MESH,
-        ).start()
-        return carry
-
-    lax.fori_loop(1, members, send_final, 0)
-    all_members(9, whole, whole).wait_recv()
+    start_plane(WHOLE, lambda q, t: final, whole.at[me_p])
+    all_plane(WHOLE, whole).wait_recv()
     whole[me_p] = final[...]
     for q in range(PLANE):
         for t in range(tp):
@@ -392,14 +427,15 @@
                 whole[q * tp + t].astype(WIDE)
             )
 
-    for phase in [*rows_of, *slots_of, stats_of, dots_of]:
+    for phase in [*tensor_of, stats_of, dots_of]:
         drain_tensor(*phase)
-    for k in range(len(lots)):
-        all_dp(k, send_slots.at[k], recv_slots.at[k]).wait_send()
-    for k in range(1, depth):
-        piece_copy(k, me_z).wait_send()
-    all_members(8, part, part_in).wait_send()
-    all_members(9, whole, whole).wait_send()
+    for phase in [*z_of, piece_of]:
+        drain_z(*phase)
+    for k in range(ways):
+        all_plane(k, full_out.at[k]).wait_send()
+        all_plane(ways + k, back_recv.at[k]).wait_send()
+    all_plane(PART, part_in).wait_send()
+    all_plane(WHOLE, whole).wait_send()
 
 
 def finish(*refs):
@@ -419,7 +455,7 @@
     own, _, inner = w_in.shape
     n, slots, group = images * seq, dp * own, own * images
     c = dp * group
-    members, high, lots = PLANE * tp, slots // PLANE, 4 * own
+    members, depth, high, ways = PLANE * tp, dp // PLANE, slots // PLANE, 2 * own
     vmem, hbm = pltpu.VMEM, pl.BlockSpec(memory_space=pltpu.HBM)
     here = pl.BlockSpec(memory_space=pltpu.VMEM)
     shapes = [((n, width), LOW), ((slots, width), WIDE), (w_in.shape, LOW), (w_out.shape, LOW)]
@@ -435,20 +471,26 @@
             vmem((c, width), LOW),
             vmem((c, n), WIDE), vmem((c, n), WIDE), vmem((c, n), WIDE),
             vmem((c, LANES), WIDE),
-            vmem((lots, tp, dp, images, LANES), LOW), vmem((lots, tp, dp, images, LANES), LOW),
-            vmem((lots, dp, images, LANES), LOW), vmem((lots, dp, images, LANES), LOW),
-            vmem((lots, tp, dp, images, LANES), LOW),
+            vmem((ways, tp, dp, images, LANES), LOW), vmem((ways, tp, dp, images, LANES), LOW),
+            vmem((ways, members, depth, images, LANES), LOW),
+            vmem((ways, members, depth, images, LANES), LOW),
+            vmem((2 * ways, depth, PLANE, images, LANES), LOW),
+            vmem((ways, PLANE, depth, images, LANES), LOW),
+            vmem((ways, depth, PLANE, images, LANES), LOW),
+            vmem((ways, members, depth, images, LANES), LOW),
+            vmem((ways, tp, depth, PLANE, images, LANES), LOW),
             vmem((2, 2, c, width), LOW),
             vmem((own, c // own, inner), LOW), vmem((own, c // own, inner), LOW),
             vmem((8, c), WIDE), vmem((tp, 8, c), WIDE),
             vmem((8, c), WIDE), vmem((tp, 8, c), WIDE),
             vmem((members, high, LANES), LOW), vmem((members, high, LANES), LOW),
-            vmem((high, LANES), WIDE), vmem((dp // PLANE, high, LANES), WIDE),
+            vmem((high, LANES), WIDE), vmem((depth, high, LANES), WIDE),
             vmem((members, high, LANES), LOW), vmem((high, LANES), LOW),
             pltpu.SemaphoreType.DMA((5,)),
-            pltpu.SemaphoreType.DMA((2 * lots + 2, tp)), pltpu.SemaphoreType.DMA((2 * lots + 2, tp)),
-            pltpu.SemaphoreType.DMA((lots + 2,)), pltpu.SemaphoreType.DMA((lots + 2,)),
-            pltpu.SemaphoreType.DMA((dp // PLANE,)), pltpu.SemaphoreType.DMA((dp // PLANE,)),
+            pltpu.SemaphoreType.DMA((2 * ways + 2, tp)), pltpu.SemaphoreType.DMA((2 * ways + 2, tp)),
+            pltpu.SemaphoreType.DMA((2 * ways + 2,)), pltpu.SemaphoreType.DMA((2 * ways + 2,)),
+            pltpu.SemaphoreType.DMA((2 * ways + 1, depth)),
+            pltpu.SemaphoreType.DMA((2 * ways + 1, depth)),
         ],
         compiler_params=pltpu.CompilerParams(
             collective_id=0, has_side_effects=True, vmem_limit_bytes=61400000

time: 90.1 us -> 84.2 us (0.935)
  Pallas kernels: 89.4 us -> 83.5 us
    pallas_call x1, Pallas kernels: 87.1 us -> 81.1 us  [on_device(): pl.pallas_call(functools.partial(kernel, tp, dp, images, own), name='moe_...]
where the time goes in v5:
time: 84.2 us; the launch traced here: 84.1 us
  Pallas kernels  83.5 us (99%)
    pallas_call x1, Pallas kernels, on_device(): pl.pallas_call(functools.partial(kernel, tp, dp, images, own), name='moe_...  81.1 us
    pallas_call x1, Pallas kernels, on_device(): pl.pallas_call(finish, name='finish', out_shape=tuple((jax.ShapeDtypeStru...  2.33 us

profile of v5, /device:TPU:1, one launch (start us, length us, event | category | flops | bytes accessed | tf_op | source)
XLA Modules:
  0.0 84.1 jit_solution(549076355762245154)
XLA Ops:
  0.6 81.1 %moe_back.1 = (bf16[288,1024]{1,0:T(8,128)(2,1)S(1)}, f32[64,1024]{1,0:T(8,128)S(1)}, bf16[2,1024,512]{2,1,0:T(8,128)(2,1)S(1)}, bf16[2,512,1024]{2,1,0:T(8,128)(2,1)S(1)}) custom-call(bf16[64,1024]{1,0:T(8,128)(2,1)} %bitcast.7, bf16[288,1024]{1,0:T(8,128)(2,1)} %bitcast.5, bf16[288,1024]{1,0:T(8,128)(2,1)} %bitcast.6, bf16[2,1024,512]{2,1,0:T(8,128)(2,1)} %w_in_hbm.1, ...), custom_call_target="tpu_custom_call" | custom-call | tf_op jit(solution)/shard_map/moe_back/pallas_call | solution.py:462
  81.8 2.3 %finish.1 = (bf16[288,1024]{1,0:T(8,128)(2,1)}, f32[64,1024]{1,0:T(8,128)}, bf16[2,1024,512]{2,1,0:T(8,128)(2,1)}, bf16[2,512,1024]{2,1,0:T(8,128)(2,1)}) custom-call(bf16[288,1024]{1,0:T(8,128)(2,1)S(1)} %get-tuple-element.12.refs_0_, f32[64,1024]{1,0:T(8,128)S(1)} %get-tuple-element.13.refs_1_, bf16[2,1024,512]{2,1,0:T(8,128)(2,1)S(1)} %get-tuple-element.14.refs_2_, ...), custom_call_target="tpu_custom_call" | custom-call | tf_op jit(solution)/shard_map/finish/pallas_call | solution.py:501

commit v6 on v5

--- a/solution.py
+++ b/solution.py
@@ -58,37 +58,29 @@
     me_z, me_q = me_d // PLANE, lax.rem(me_d, PLANE)
     me_p = me_q * tp + me_t
 
-    def copy_tensor(phase, k, src, dst, slot):
-        to = lax.rem(me_t + k, tp)
-        return pltpu.make_async_remote_copy(
-            src_ref=src(to), dst_ref=dst(slot),
-            send_sem=t_send.at[phase, k], recv_sem=t_recv.at[phase, k],
-            device_id={"tensor": to}, device_id_type=MESH,
-        )
-
-    def start_tensor(phase, src, dst):
-        for k in sorted(range(1, tp), key=lambda k: -min(k, tp - k)):
-            copy_tensor(phase, k, src, dst, me_t).start()
-
-    def before(k):
-        return lax.rem(me_t + tp - k, tp)
-
-    def await_one(k, phase, src, dst):
-        copy_tensor(phase, k, src, dst, before(k)).wait_recv()
-
-    def await_tensor(phase, src, dst):
-        for k in range(1, tp):
-            await_one(k, phase, src, dst)
-
-    def drain_tensor(phase, src, dst):
-        for k in range(1, tp):
-            copy_tensor(phase, k, src, dst, me_t).wait_send()
-
     def remote(src, dst, send_sem, recv_sem, where):
         return pltpu.make_async_remote_copy(
             src_ref=src, dst_ref=dst, send_sem=send_sem, recv_sem=recv_sem,
             device_id=where, device_id_type=MESH,
         )
+
+    def outward(size):
+        return sorted(range(1, size), key=lambda k: -min(k, size - k))
+
+    def start_tensor(phase, src, dst, bulk):
+        for k in outward(tp):
+            to = lax.rem(me_t + k, tp)
+            remote(
+                src(to), dst, t_send.at[phase], t_recv.at[phase], {"tensor": to}
+            ).start()
+
+    def all_tensor(phase, src, dst, bulk):
+        return remote(
+            bulk, bulk, t_send.at[phase], t_recv.at[phase], {"tensor": lax.rem(me_t + 1, tp)}
+        )
+
+    def before(k):
+        return lax.rem(me_t + tp - k, tp)
 
     near = [
         (lax.rem(me_q + jq, PLANE), lax.rem(me_t + jt, tp))
@@ -105,41 +97,38 @@
             ).start()
 
     def all_plane(phase, blocks):
-        few = pl.ds(0, members - 1)
+        few = blocks.at[pl.ds(0, members - 1)]
         q, t = near[0]
         return remote(
-            blocks.at[few], blocks.at[few], p_send.at[phase], p_recv.at[phase],
-            {"dp": me_z * PLANE + q, "tensor": t},
-        )
-
-    def z_copy(phase, k, src, dst, slot):
-        to = lax.rem(me_z + k, depth)
+            few, few, p_send.at[phase], p_recv.at[phase], {"dp": me_z * PLANE + q, "tensor": t}
+        )
+
+    def start_z(phase, src, dst, bulk):
+        for k in outward(depth):
+            to = lax.rem(me_z + k, depth)
+            remote(
+                src(to), dst, z_send.at[phase], z_recv.at[phase], {"dp": to * PLANE + me_q}
+            ).start()
+
+    def all_z(phase, src, dst, bulk):
+        to = lax.rem(me_z + 1, depth)
         return remote(
-            src(to), dst(slot), z_send.at[phase, k], z_recv.at[phase, k],
-            {"dp": to * PLANE + me_q},
-        )
-
-    def start_z(phase, src, dst):
-        for k in sorted(range(1, depth), key=lambda k: -min(k, depth - k)):
-            z_copy(phase, k, src, dst, me_z).start()
-
-    def await_z(phase, src, dst):
-        for k in range(1, depth):
-            z_copy(phase, k, src, dst, lax.rem(me_z + depth - k, depth)).wait_recv()
-
-    def drain_z(phase, src, dst):
-        for k in range(1, depth):
-            z_copy(phase, k, src, dst, me_z).wait_send()
+            bulk, bulk, z_send.at[phase], z_recv.at[phase], {"dp": to * PLANE + me_q}
+        )
 
     lots = [(turn, kind, e) for turn in range(2) for kind in range(2) for e in range(own)]
     number = {lot: k for k, lot in enumerate(lots)}
     STATS, DOTS = len(lots), len(lots) + 1
     ways = len(lots) // 2
+    few_t, few_z = pl.ds(0, tp - 1), pl.ds(0, depth - 1)
     tensor_of = [
-        (k, lambda to, k=k: out_send.at[k, to], lambda s, k=k: out_recv.at[k, s])
+        (k, lambda to, k=k: out_send.at[k, to], out_recv.at[k, me_t], out_recv.at[k, few_t])
         for k in range(ways)
     ] + [
-        (ways + k, lambda to, k=k: slots_back.at[k], lambda s, k=k: full_back.at[k, s])
+        (
+            ways + k, lambda to, k=k: slots_back.at[k], full_back.at[k, me_t],
+            full_back.at[k, few_t],
+        )
         for k in range(ways)
     ]
     plane_of = [
@@ -149,15 +138,21 @@
         for k in range(ways)
     ]
     z_of = [
-        (k, lambda to, k=k: send_slots.at[k, to], lambda s, k=k: slots_out.at[k, :, s])
+        (
+            k, lambda to, k=k: send_slots.at[k, to], slots_out.at[k, :, me_z],
+            send_slots.at[k, few_z],
+        )
         for k in range(ways)
     ] + [
-        (k, lambda to, k=k: send_slots.at[k, to], lambda s, k=k: slots_back.at[k - ways, s])
-        for k in range(ways, 2 * ways)
+        (
+            ways + k, lambda to, k=k: send_slots.at[ways + k, to], slots_back.at[k, me_z],
+            slots_back.at[k, few_z],
+        )
+        for k in range(ways)
     ]
     PART, WHOLE, PIECE = 2 * ways, 2 * ways + 1, 2 * ways
-    stats_of = (STATS, lambda to: stats, lambda s: stats_in.at[s])
-    dots_of = (DOTS, lambda to: dots, lambda s: dots_in.at[s])
+    stats_of = (STATS, lambda to: stats, stats_in.at[me_t], stats_in.at[few_t])
+    dots_of = (DOTS, lambda to: dots, dots_in.at[me_t], dots_in.at[few_t])
 
     loads = [
         pltpu.make_async_copy(src, dst, local_sem.at[k])
@@ -173,7 +168,7 @@
 
     barrier = pltpu.get_barrier_semaphore()
 
-    for k in sorted(range(1, depth), key=lambda k: -min(k, depth - k)):
+    for k in outward(depth):
         pl.semaphore_signal(
             barrier, inc=1, device_id={"dp": lax.rem(me_z + k, depth) * PLANE + me_q},
             device_id_type=MESH,
@@ -247,7 +242,7 @@
     for e in range(own):
         begin_sum(plain(share_low[e * half:(e + 1) * half], cot[...]), (0, 1, e))
 
-    await_tensor(*stats_of)
+    all_tensor(*stats_of).wait_recv()
     stats_in[me_t] = stats[...]
     most = stats_in[0, 0:1]
     for s in range(1, tp):
@@ -270,10 +265,10 @@
     def pass_on(lot):
         k, e = number[lot], lot[2]
         if lot[0] == 0:
+            all_tensor(*tensor_of[k]).wait_recv()
             total_rows = None
             for back in range(tp):
                 if back:
-                    await_one(back, *tensor_of[k])
                     term = out_recv[k, before(back)]
                 else:
                     term = out_send[k, me_t]
@@ -296,7 +291,7 @@
 
     def gather(lot):
         k = number[lot]
-        await_z(*z_of[k])
+        all_z(*z_of[k]).wait_recv()
         if lot[0] == 0:
             slots_out[k, :, me_z] = send_slots[k, me_z]
             start_plane(*plane_of[k])
@@ -315,7 +310,7 @@
                     block = full_out[k, q * tp + t].astype(WIDE).reshape(across, LANES)
                     flat[turn, kind, rows, t * LANES:(t + 1) * LANES] = block.astype(LOW)
         else:
-            await_tensor(*tensor_of[k])
+            all_tensor(*tensor_of[k]).wait_recv()
             full_back[k - ways, me_t] = slots_back[k - ways]
             for t in range(tp):
                 block = full_back[k - ways, t].astype(WIDE).reshape(half, LANES)
@@ -385,7 +380,7 @@
         [rows_by_rows(assembled((1, 1, e)), tok[...]) for e in range(own)]
     )
     slot_grad = flat[1, 1]
-    await_tensor(*dots_of)
+    all_tensor(*dots_of).wait_recv()
     dots_in[me_t] = dots[...]
     dot_line = dots_in[0, 0:1]
     for s in range(1, tp):
@@ -413,9 +408,9 @@
     all_plane(PART, part_in).wait_recv()
     part_in[me_p] = part[me_p]
     piece[...] = jnp.sum(part_in[...].astype(WIDE), axis=0)
-    piece_of = (PIECE, lambda to: piece, lambda s: piece_in.at[s])
+    piece_of = (PIECE, lambda to: piece, piece_in.at[me_z], piece_in.at[few_z])
     start_z(*piece_of)
-    await_z(*piece_of)
+    all_z(*piece_of).wait_recv()
     piece_in[me_z] = piece[...]
     final[...] = jnp.sum(piece_in[...], axis=0).astype(LOW)
     start_plane(WHOLE, lambda q, t: final, whole.at[me_p])
@@ -428,9 +423,9 @@
             )
 
     for phase in [*tensor_of, stats_of, dots_of]:
-        drain_tensor(*phase)
+        all_tensor(*phase).wait_send()
     for phase in [*z_of, piece_of]:
-        drain_z(*phase)
+        all_z(*phase).wait_send()
     for k in range(ways):
         all_plane(k, full_out.at[k]).wait_send()
         all_plane(ways + k, back_recv.at[k]).wait_send()
@@ -487,10 +482,9 @@
             vmem((high, LANES), WIDE), vmem((depth, high, LANES), WIDE),
             vmem((members, high, LANES), LOW), vmem((high, LANES), LOW),
             pltpu.SemaphoreType.DMA((5,)),
-            pltpu.SemaphoreType.DMA((2 * ways + 2, tp)), pltpu.SemaphoreType.DMA((2 * ways + 2, tp)),
             pltpu.SemaphoreType.DMA((2 * ways + 2,)), pltpu.SemaphoreType.DMA((2 * ways + 2,)),
-            pltpu.SemaphoreType.DMA((2 * ways + 1, depth)),
-            pltpu.SemaphoreType.DMA((2 * ways + 1, depth)),
+            pltpu.SemaphoreType.DMA((2 * ways + 2,)), pltpu.SemaphoreType.DMA((2 * ways + 2,)),
+            pltpu.SemaphoreType.DMA((2 * ways + 1,)), pltpu.SemaphoreType.DMA((2 * ways + 1,)),
         ],
         compiler_params=pltpu.CompilerParams(
             collective_id=0, has_side_effects=True, vmem_limit_bytes=61400000

time: 84.2 us -> 81 us (0.962)
  Pallas kernels: 83.5 us -> 80.3 us
    pallas_call x1, Pallas kernels: 81.1 us -> 78 us  [on_device(): pl.pallas_call(functools.partial(kernel, tp, dp, images, own), name='moe_...]
where the time goes in v6:
time: 81 us
  Pallas kernels  80.3 us (99%)
    pallas_call x1, Pallas kernels, on_device(): pl.pallas_call(functools.partial(kernel, tp, dp, images, own), name='moe_...  78 us
    pallas_call x1, Pallas kernels, on_device(): pl.pallas_call(finish, name='finish', out_shape=tuple((jax.ShapeDtypeStru...  2.33 us

profile of v6, /device:TPU:1, one launch (start us, length us, event | category | flops | bytes accessed | tf_op | source)
XLA Modules:
  0.0 81.0 jit_solution(828813434016409815)
XLA Ops:
  0.6 78.0 %moe_back.1 = (bf16[288,1024]{1,0:T(8,128)(2,1)S(1)}, f32[64,1024]{1,0:T(8,128)S(1)}, bf16[2,1024,512]{2,1,0:T(8,128)(2,1)S(1)}, bf16[2,512,1024]{2,1,0:T(8,128)(2,1)S(1)}) custom-call(bf16[64,1024]{1,0:T(8,128)(2,1)} %bitcast.7, bf16[288,1024]{1,0:T(8,128)(2,1)} %bitcast.5, bf16[288,1024]{1,0:T(8,128)(2,1)} %bitcast.6, bf16[2,1024,512]{2,1,0:T(8,128)(2,1)} %w_in_hbm.1, ...), custom_call_target="tpu_custom_call" | custom-call | tf_op jit(solution)/shard_map/moe_back/pallas_call | solution.py:457
  78.6 2.3 %finish.1 = (bf16[288,1024]{1,0:T(8,128)(2,1)}, f32[64,1024]{1,0:T(8,128)}, bf16[2,1024,512]{2,1,0:T(8,128)(2,1)}, bf16[2,512,1024]{2,1,0:T(8,128)(2,1)}) custom-call(bf16[288,1024]{1,0:T(8,128)(2,1)S(1)} %get-tuple-element.12.refs_0_, f32[64,1024]{1,0:T(8,128)S(1)} %get-tuple-element.13.refs_1_, bf16[2,1024,512]{2,1,0:T(8,128)(2,1)S(1)} %get-tuple-element.14.refs_2_, ...), custom_call_target="tpu_custom_call" | custom-call | tf_op jit(solution)/shard_map/finish/pallas_call | solution.py:495
